TPU v7x, 32 devices: a whole 2x2x4 slice. The times are simulated.
32 devices in a mesh: groups: 2 (over x), freq: 16 (over z, y, core).
Axes of the slice: x: 2, y: 2, z: 4, core: 2. Of those that a mesh axis runs over, the one named last changes fastest.
Arguments:
- traces: bfloat16 [1024, 2048, 32], P('freq', None, 'groups'), parts along dimension 2, may hold values from -6 to 6
- freq_index: int32 [16], replicated, may hold values from 1 to 511
- block_map: int32 [64, 64], replicated, may hold values 0 or 1
- green_rec: bfloat16 [16, 2, 2048, 1536], P('freq', None, None, 'groups'), parts along dimension 3, may hold values from -0.1875 to 0.1875
- green_src: bfloat16 [16, 2, 16, 1536], P('freq', None, None, 'groups'), parts along dimension 3, may hold values from -0.25 to 0.25
Outputs:
- image: float32 [1536], P(('groups', 'freq')), parts along dimension 0
There are 2 independent parts, one for each index of `groups`. A program takes and returns all parts, laid end to end along the dimension named above; an argument that names none is the same for every part. Nothing has to cross between parts.
Inputs may be any that keep to these rules, and one draw needn't show every extreme that they name: `freq_index`: frequency bins; they may repeat. `block_map`: 1 where a receiver block lies in an image tile's aperture.
All inputs are finite; a program needn't handle non-finite values.
Results may differ from a plain program's by a relative error of at most 0.0038.
Values may be sent and summed in bfloat16 or wider, within the bound.
A program may use at most 64 MiB of HBM per device.

v0:
```python
import functools
import math

import jax
import jax.numpy as jnp
from jax import lax
from jax.experimental import pallas as pl
from jax.experimental.pallas import tpu as pltpu
from jax.sharding import PartitionSpec as P


def dft_table(freq_index, length):
    sample_index = jnp.arange(length, dtype=jnp.int32)
    phases = freq_index[:, None] * sample_index[None, :] % length
    angles = phases.astype(jnp.float32) * jnp.float32(2.0 * math.pi / length)
    stacked = jnp.stack((jnp.cos(angles), -jnp.sin(angles)), axis=1)
    return stacked.reshape(freq_index.shape[0] * 2, length).astype(jnp.bfloat16)


def expand_map(block_map, receivers, points):
    row_span = receivers // block_map.shape[0]
    col_span = points // block_map.shape[1]
    return jnp.repeat(jnp.repeat(block_map, row_span, axis=0), col_span, axis=1).astype(
        jnp.bfloat16
    )


def transform(cos_table, records, length):
    spectrum = jnp.dot(cos_table, records.reshape(length, -1), preferred_element_type=jnp.float32)
    return (spectrum * (1.0 / math.sqrt(length))).astype(jnp.bfloat16)


def back_project(spectra, masked):
    swapped = jnp.stack((spectra[:, 1], -spectra[:, 0]), axis=1)
    blocks = jnp.stack((spectra, swapped), axis=1)
    return jnp.einsum("fcrx,focrs->fosx", masked, blocks, preferred_element_type=jnp.float32)


def body(traces, freq_index, block_map, green_rec, green_src):
    shards = lax.axis_size("freq")
    length = traces.shape[0] * shards
    receivers = traces.shape[1]
    shots = traces.shape[2]
    freqs = freq_index.shape[0]
    cos_table = dft_table(freq_index, length)
    masked = green_rec * expand_map(block_map, receivers, green_rec.shape[3])[None, None]
    regrouped = lax.all_to_all(traces, "freq", split_axis=2, concat_axis=0, tiled=True)
    spectrum = transform(cos_table, regrouped, length).reshape(freqs, 2, receivers, shots // shards)
    gathered = lax.all_to_all(spectrum, "freq", split_axis=0, concat_axis=3, tiled=True)
    back_field = back_project(gathered, masked)
    partial_image = jnp.sum(green_src.astype(jnp.float32) * back_field, axis=(0, 1, 2))
    return lax.psum_scatter(partial_image, "freq", scatter_dimension=0, tiled=True)


CORES = 2
ROWS = 2
LAG = 4
LANES = 128


def bands(half):
    return tuple((start, LANES) for start in range(0, half, LANES))


def seat(cols, row, core):
    return (cols * ROWS + row) * CORES + core


def remote(src, dst, send_sem, recv_sem, target):
    return pltpu.make_async_remote_copy(
        src_ref=src,
        dst_ref=dst,
        send_sem=send_sem,
        recv_sem=recv_sem,
        device_id={"freq": target},
        device_id_type=pl.DeviceIdType.MESH,
    )


def imaging_kernel(
    shots,
    x_ref,
    fi_hbm,
    map_ref,
    green_ref,
    src_ref,
    out_ref,
    fi_ref,
    x_all,
    x_far,
    table,
    y_send,
    y_own,
    y_recv,
    z_send,
    z_own,
    z_recv,
    green_v,
    src_v,
    map_v,
    mask_v,
    acc,
    i_send,
    i_recv,
    x_sem,
    load_sem,
    far_send,
    far_recv,
    ys_sem,
    yr_sem,
    zs_sem,
    zr_sem,
    is_sem,
    ir_sem,
    up_sem,
    down_sem,
    pair_sem,
    row_sem,
):
    shards = i_send.shape[0]
    cols = shards // (ROWS * CORES)
    local_rows, half = x_far.shape
    samples = local_rows // shots
    length = samples * shards
    band = y_own.shape[0]
    steps = bands(half)
    chunks = len(steps)
    freqs = fi_ref.shape[0]
    receivers = CORES * half
    points = acc.shape[1]
    block = 2 * shots
    bf16, f32 = jnp.bfloat16, jnp.float32

    me = lax.axis_index("freq")
    core = lax.rem(me, CORES)
    row = lax.rem(me // CORES, ROWS)
    col = me // (CORES * ROWS)
    mate = seat(col, row, 1 - core)
    across = seat(col, 1 - row, core)

    barrier = pltpu.get_barrier_semaphore()

    def tell(sem, target):
        pl.semaphore_signal(
            sem, inc=1, device_id={"freq": target}, device_id_type=pl.DeviceIdType.MESH
        )

    tell(barrier, mate)
    tell(barrier, across)

    @pl.when(col > 0)
    def _():
        tell(barrier, seat(col - 1, row, core))

    @pl.when(col < cols - 1)
    def _():
        tell(barrier, seat(col + 1, row, core))

    def relay(hop):
        @pl.when(col == hop)
        def _():
            if hop > 0:
                pl.semaphore_wait(up_sem, 1)
            if hop < cols - 1:
                tell(up_sem, seat(col + 1, row, core))

        @pl.when(col == cols - 1 - hop)
        def _():
            if hop > 0:
                pl.semaphore_wait(down_sem, 1)
            if hop < cols - 1:
                tell(down_sem, seat(col - 1, row, core))

    def lanes(core_at, k):
        return pl.ds(pl.multiple_of(core_at * half + steps[k][0], LANES), steps[k][1])

    def x_load(core_at):
        side = pl.ds(pl.multiple_of(core_at * half, LANES), half)
        return pltpu.make_async_copy(x_ref.at[:, side], x_all.at[:, side], x_sem.at[core_at])

    def far_copy(k):
        return remote(
            x_all.at[:, lanes(1 - core, k)],
            x_far.at[:, pl.ds(*steps[k])],
            far_send,
            far_recv.at[k],
            mate,
        )

    fi_load = pltpu.make_async_copy(fi_hbm, fi_ref, load_sem.at[3])
    map_load = pltpu.make_async_copy(map_ref, map_v, load_sem.at[0])
    src_load = pltpu.make_async_copy(src_ref, src_v, load_sem.at[1])
    green_load = pltpu.make_async_copy(green_ref, green_v, load_sem.at[2])
    fi_load.start()
    x_load(1 - core).start()
    x_load(core).start()
    map_load.start()
    src_load.start()
    green_load.start()

    table_rows = 2 * freqs
    span = CORES * samples
    line = lax.broadcasted_iota(jnp.int32, (table_rows, span), 0)
    column = lax.broadcasted_iota(jnp.int32, (table_rows, span), 1)
    fi_load.wait()
    bins = jnp.zeros((table_rows, span), jnp.int32)
    for f in range(freqs):
        place = ((f // CORES) % ROWS * cols + f // (CORES * ROWS)) * CORES + f % CORES
        bins = jnp.where(line // 2 == place, fi_ref[f], bins)
    time = jnp.where(column < samples, me * samples + column, (mate - 1) * samples + column)
    angles = lax.rem(bins * time, length).astype(f32) * f32(2.0 * math.pi / length)
    small = jnp.where(line % 2 == 0, jnp.cos(angles), -jnp.sin(angles)).astype(bf16)
    wide = span * shots
    spread = lax.broadcasted_iota(jnp.int32, (span, wide), 1) // shots == lax.broadcasted_iota(
        jnp.int32, (span, wide), 0
    )
    stretched = jnp.dot(small, jnp.where(spread, 1.0, 0.0).astype(bf16), preferred_element_type=f32)
    same_shot = lax.broadcasted_iota(jnp.int32, (shots, wide), 1) % shots == lax.broadcasted_iota(
        jnp.int32, (shots, wide), 0
    )
    for r in range(table_rows):
        spread_row = jnp.broadcast_to(stretched[r : r + 1, :], (shots, wide))
        table[r * shots : (r + 1) * shots, :] = jnp.where(same_shot, spread_row, 0.0).astype(bf16)

    greeted = 2 + jnp.minimum(col, 1) + jnp.minimum(cols - 1 - col, 1)
    pl.semaphore_wait(barrier, greeted)
    x_load(1 - core).wait()
    for k in range(chunks):
        far_copy(k).start()

    def partial(side, k):
        rows = pl.ds(pl.multiple_of(side * band, band), band)
        at = pl.ds(*steps[k])
        near = jnp.dot(table[rows, :local_rows], x_all[:, lanes(core, k)], preferred_element_type=f32)
        return near + jnp.dot(table[rows, local_rows:], x_far[:, at], preferred_element_type=f32)

    def y_copy(k):
        at = pl.ds(*steps[k])
        return remote(y_send.at[:, at], y_recv.at[:, at], ys_sem, yr_sem.at[k], across)

    def send_partial(k):
        far_copy(k).wait_recv()
        y_send[:, pl.ds(*steps[k])] = partial(1 - row, k).astype(bf16)
        y_copy(k).start()

    def keep_partial(k):
        y_own[:, pl.ds(*steps[k])] = partial(row, k)

    def block_rows(col_at, core_at):
        return pl.ds(pl.multiple_of((col_at * CORES + core_at) * block, block), block)

    peers = [(dc, dk) for dc in range(cols) for dk in range(CORES) if dc or dk]

    def z_copy(k, dc, dk):
        to_col = lax.rem(col + dc, cols)
        to_core = lax.rem(core + dk, CORES)
        return remote(
            z_send.at[block_rows(to_col, to_core), pl.ds(*steps[k])],
            z_recv.at[col, :, lanes(core, k)],
            zs_sem,
            zr_sem.at[k],
            seat(to_col, row, to_core),
        )

    def scatter(k):
        y_copy(k).wait_recv()
        at = pl.ds(*steps[k])
        y_own[:, at] = y_own[:, at] + y_recv[:, at].astype(f32)
        z_send[:, at] = y_own[:, at].astype(bf16)
        for dc, dk in peers:
            z_copy(k, dc, dk).start()
        z_own[:, at] = y_own[block_rows(col, core), at]
    x_load(core).wait()
    relay(0)
    for k in range(chunks):
        send_partial(k)
        if k % 2 == 1 and (k + 1) // 2 < cols:
            relay((k + 1) // 2)
        if k % 4 == 3:
            keep_partial(k // 4)
    early = (chunks + 3) // 4
    for k in range(chunks // 4, early):
        keep_partial(k)
    for hop in range(chunks // 2 + 1, cols):
        relay(hop)
    tell(pair_sem, mate)
    pl.semaphore_wait(pair_sem, 1)
    tell(row_sem, across)
    scatter(0)
    keep_partial(early)
    scatter(1)
    for k in range(early + 1, min(early + 2, chunks)):
        keep_partial(k)

    map_load.wait()
    tiles = map_v.shape[1]
    in_tile = lax.broadcasted_iota(jnp.int32, (tiles, points), 1) // (
        points // tiles
    ) == lax.broadcasted_iota(jnp.int32, (tiles, points), 0)
    mask_v[...] = jnp.dot(
        map_v[...].astype(f32).astype(bf16),
        jnp.where(in_tile, 1.0, 0.0).astype(bf16),
        preferred_element_type=f32,
    )
    green_load.wait()
    deep = receivers // map_v.shape[0]

    def mask_block(i, carry):
        seen = jnp.broadcast_to(mask_v[pl.ds(i, 1), :], (deep, points)).astype(bf16)
        for part in range(2):
            at = pl.ds(pl.multiple_of(part * receivers + i * deep, deep), deep)
            green_v[at, :] = green_v[at, :] * seen
        return carry

    lax.fori_loop(0, map_v.shape[0], mask_block, 0)
    acc[...] = jnp.zeros_like(acc)

    def z_arrival(k):
        every = z_send.at[pl.ds(0, len(peers) * block), pl.ds(*steps[k])]
        return pltpu.make_async_copy(every, every, zr_sem.at[k])

    def use(spectrum, core_at, k):
        spectrum = spectrum * f32(1.0 / math.sqrt(length))
        turned = jnp.concatenate((spectrum[shots:], -spectrum[:shots]), axis=0)
        first = lanes(core_at, k)
        second = lanes(CORES + core_at, k)
        acc[...] += jnp.dot(
            spectrum.astype(bf16), green_v[first, :], preferred_element_type=f32
        ) + jnp.dot(turned.astype(bf16), green_v[second, :], preferred_element_type=f32)

    def consume(k):
        z_arrival(k).wait()
        for dk in range(CORES):
            from_core = lax.rem(core + dk, CORES)
            total = None if dk else z_own[:, pl.ds(*steps[k])]
            for dc in range(cols):
                if dc or dk:
                    from_col = lax.rem(col + cols - dc, cols)
                    term = z_recv[from_col, :, lanes(from_core, k)].astype(f32)
                    total = term if total is None else total + term
            use(total, from_core, k)

    for k in range(2, chunks):
        scatter(k)
        for at in range(early + 2 * k - 2, min(early + 2 * k, chunks)):
            keep_partial(at)
        if k >= LAG:
            consume(k - LAG)
    for k in range(chunks - LAG, chunks):
        consume(k)

    src_load.wait()
    product = src_v[...].astype(f32) * acc[...]
    folded = product[0:8]
    for at in range(8, block, 8):
        folded = folded + product[at : at + 8]
    flat = jnp.broadcast_to(jnp.sum(folded, axis=0, keepdims=True), (8, points))
    each = points // shards
    for d in range(shards):
        i_send[d] = pltpu.roll(flat, (points - d * each) % points, 1)[0:1, :LANES]

    def i_copy(step):
        to = lax.rem(me + step, shards)
        return remote(i_send.at[to], i_recv.at[step], is_sem, ir_sem, to)

    pl.semaphore_wait(row_sem, 1)
    for step in range(1, shards):
        i_copy(step).start()
    total = i_send[me]
    others = i_recv.at[pl.ds(1, shards - 1)]
    pltpu.make_async_copy(others, others, ir_sem).wait()
    for step in range(1, shards):
        total = total + i_recv[step]
    out_ref[...] = total

    z_sent = z_send.at[pl.ds(0, len(peers) * block), :]
    for sent, sem in ((x_far, far_send), (y_send, ys_sem), (z_sent, zs_sem), (others, is_sem)):
        pltpu.make_async_copy(sent, sent, sem).wait()


def fused_body(traces, freq_index, block_map, green_rec, green_src):
    shards = lax.axis_size("freq")
    samples, receivers, shots = traces.shape
    points = green_rec.shape[3]
    freqs = freq_index.shape[0]
    cols = shards // (ROWS * CORES)
    half = receivers // CORES
    chunks = len(bands(half))
    records = jnp.transpose(traces, (0, 2, 1)).reshape(samples * shots, receivers)
    green = green_rec.reshape(2 * receivers, points)
    sources = green_src.reshape(2 * shots, points)
    band = 2 * freqs * shots // ROWS
    block = 2 * shots
    bf16, f32 = jnp.bfloat16, jnp.float32
    dma = pltpu.SemaphoreType.DMA
    outside = pl.BlockSpec(memory_space=pltpu.HBM)
    image = pl.pallas_call(
        functools.partial(imaging_kernel, shots),
        out_shape=jax.ShapeDtypeStruct((1, LANES), f32),
        in_specs=[outside] * 5,
        out_specs=pl.BlockSpec(memory_space=pltpu.VMEM),
        scratch_shapes=[
            pltpu.SMEM(freq_index.shape, jnp.int32),
            pltpu.VMEM((samples * shots, receivers), bf16),
            pltpu.VMEM((samples * shots, half), bf16),
            pltpu.VMEM((2 * freqs * shots, CORES * samples * shots), bf16),
            pltpu.VMEM((band, half), bf16),
            pltpu.VMEM((band, half), f32),
            pltpu.VMEM((band, half), bf16),
            pltpu.VMEM((band, half), bf16),
            pltpu.VMEM((block, half), f32),
            pltpu.VMEM((cols, block, receivers), bf16),
            pltpu.VMEM((2 * receivers, points), bf16),
            pltpu.VMEM((block, points), bf16),
            pltpu.VMEM(block_map.shape, jnp.int32),
            pltpu.VMEM((block_map.shape[0], points), f32),
            pltpu.VMEM((block, points), f32),
            pltpu.VMEM((shards, 1, LANES), f32),
            pltpu.VMEM((shards, 1, LANES), f32),
            dma((CORES,)),
            dma((4,)),
            dma,
            dma((chunks,)),
            dma,
            dma((chunks,)),
            dma,
            dma((chunks,)),
            dma,
            dma,
        ]
        + [pltpu.SemaphoreType.REGULAR] * 4,
        compiler_params=pltpu.CompilerParams(
            collective_id=0, has_side_effects=True, vmem_limit_bytes=48 * 1024 * 1024
        ),
    )(
        *(
            pltpu.with_memory_space_constraint(array, pltpu.HBM)
            for array in (records, freq_index, block_map, green, sources)
        )
    )
    return image[0, : points // shards]


def moves_less(traces, freq_index, green_rec):
    shards = lax.axis_size("freq")
    samples, receivers, shots = traces.shape
    freqs = freq_index.shape[0]
    return (
        2 * freqs <= samples
        and freqs == shards
        and shards % (ROWS * CORES) == 0
        and shots % 16 == 0
        and receivers % (CORES * 4 * LANES) == 0
        and green_rec.shape[3] % LANES == 0
        and green_rec.shape[3] // shards <= LANES
    )


def chosen_body(traces, freq_index, block_map, green_rec, green_src):
    fused = moves_less(traces, freq_index, green_rec)
    return (fused_body if fused else body)(traces, freq_index, block_map, green_rec, green_src)


def solution(mesh):
    in_specs = (
        P("freq", None, "groups"),
        P(),
        P(),
        P("freq", None, None, "groups"),
        P("freq", None, None, "groups"),
    )
    out_specs = P(("groups", "freq"))
    return jax.shard_map(chosen_body, mesh=mesh, in_specs=in_specs, out_specs=out_specs, check_vma=False)
```

profile of v0, /device:TPU:0, one launch (start us, length us, event | category | flops | bytes accessed | tf_op | source)
XLA Modules:
  0.0 29.9 jit_solution(6155710515491938523)
XLA Ops:
  0.0 29.4 %shard_map.55 = f32[1,128]{1,0:T(1,128)S(1)} custom-call(bf16[1024,2048]{1,0:T(8,128)(2,1)} %bitcast.8, s32[16]{0:T(128)} %fi_hbm.1, s32[64,64]{1,0:T(8,128)} %map_ref.1, bf16[4096,768]{1,0:T(8,128)(2,1)} %bitcast.7, bf16[32,768]{1,0:T(8,128)(2,1)} %bitcast.9), custom_call_target="tpu_custom_call" | custom-call | tf_op jit(solution)/shard_map/pallas_call | solution.py:397
  29.4 0.5 %slice_bitcast_fusion = f32[48]{0:T(128)} fusion(f32[1,128]{1,0:T(1,128)S(1)} %shard_map.55), kind=kLoop, calls=%fused_computation | loop fusion | bytes 384 | tf_op jit(solution)/shard_map/squeeze | solution.py:441
where the time goes:
time: 30.1 us; the launch traced here: 29.9 us
  Pallas kernels  29.4 us (98%)
  local copies, waits for them, and re-layouts  0.51 us (2%)
    pallas_call x1, Pallas kernels, fused_body(): pl.pallas_call(functools.partial(imaging_kernel, shots), out_shape=jax.Sh...  29.4 us

commit v1 on v0

v1 whole, which is shorter than its diff:
```python
import math

import jax
import jax.numpy as jnp
from jax import lax
from jax.experimental import pallas as pl
from jax.experimental.pallas import tpu as pltpu
from jax.sharding import PartitionSpec as P


def dft_table(freq_index, length):
    sample_index = jnp.arange(length, dtype=jnp.int32)
    phases = freq_index[:, None] * sample_index[None, :] % length
    angles = phases.astype(jnp.float32) * jnp.float32(2.0 * math.pi / length)
    stacked = jnp.stack((jnp.cos(angles), -jnp.sin(angles)), axis=1)
    return stacked.reshape(freq_index.shape[0] * 2, length).astype(jnp.bfloat16)


def expand_map(block_map, receivers, points):
    row_span = receivers // block_map.shape[0]
    col_span = points // block_map.shape[1]
    return jnp.repeat(jnp.repeat(block_map, row_span, axis=0), col_span, axis=1).astype(
        jnp.bfloat16
    )


def transform(cos_table, records, length):
    spectrum = jnp.dot(cos_table, records.reshape(length, -1), preferred_element_type=jnp.float32)
    return (spectrum * (1.0 / math.sqrt(length))).astype(jnp.bfloat16)


def back_project(spectra, masked):
    swapped = jnp.stack((spectra[:, 1], -spectra[:, 0]), axis=1)
    blocks = jnp.stack((spectra, swapped), axis=1)
    return jnp.einsum("fcrx,focrs->fosx", masked, blocks, preferred_element_type=jnp.float32)


def body(traces, freq_index, block_map, green_rec, green_src):
    shards = lax.axis_size("freq")
    length = traces.shape[0] * shards
    receivers = traces.shape[1]
    shots = traces.shape[2]
    freqs = freq_index.shape[0]
    cos_table = dft_table(freq_index, length)
    masked = green_rec * expand_map(block_map, receivers, green_rec.shape[3])[None, None]
    regrouped = lax.all_to_all(traces, "freq", split_axis=2, concat_axis=0, tiled=True)
    spectrum = transform(cos_table, regrouped, length).reshape(freqs, 2, receivers, shots // shards)
    gathered = lax.all_to_all(spectrum, "freq", split_axis=0, concat_axis=3, tiled=True)
    back_field = back_project(gathered, masked)
    partial_image = jnp.sum(green_src.astype(jnp.float32) * back_field, axis=(0, 1, 2))
    return lax.psum_scatter(partial_image, "freq", scatter_dimension=0, tiled=True)


CORES = 2
ROWS = 2
PAIR = 2
LANES = 128
SUBLANES = 8
LEGS = 4


def chunks_of(half):
    first = (LANES, LANES) if half > 2 * LANES else (LANES,) * (half // LANES)
    sizes = list(first)
    while sum(sizes) < half:
        sizes.append(min(2 * LANES, half - sum(sizes)))
    return tuple((sum(sizes[:k]), size) for k, size in enumerate(sizes))


def seat(col, row, core):
    return (col * ROWS + row) * CORES + core


def remote(src, dst, send_sem, recv_sem, target):
    return pltpu.make_async_remote_copy(
        src_ref=src,
        dst_ref=dst,
        send_sem=send_sem,
        recv_sem=recv_sem,
        device_id={"freq": target},
        device_id_type=pl.DeviceIdType.MESH,
    )


def imaging_kernel(
    x_ref,
    fi_hbm,
    map_ref,
    green_ref,
    src_ref,
    out_ref,
    fi_ref,
    x_out,
    x_near,
    x_far,
    table,
    y_send,
    y_keep,
    y_recv,
    relay_send,
    relay_recv,
    cross_send,
    close_send,
    own_send,
    fin,
    green_v,
    src_v,
    map_v,
    mask_v,
    acc,
    i_send,
    i_recv,
    out_sem,
    near_sem,
    load_sem,
    green_sem,
    far_send,
    far_recv,
    ys_sem,
    yr_sem,
    rs_sem,
    rr_sem,
    cs_sem,
    ns_sem,
    os_sem,
    fin_sem,
    last_sem,
    is_sem,
    ir_sem,
    line_sem,
    pair_sem,
    row_sem,
):
    shards = i_send.shape[0]
    cols = shards // (ROWS * CORES)
    samples, folds, _, half = x_far.shape
    length = samples * shards
    steps = chunks_of(half)
    chunks = len(steps)
    freqs = fi_ref.shape[0]
    points = acc.shape[1]
    block = acc.shape[0]
    groups = 2 * folds
    depth = samples * SUBLANES
    bf16, f32 = jnp.bfloat16, jnp.float32

    me = lax.axis_index("freq")
    core = lax.rem(me, CORES)
    row = lax.rem(me // CORES, ROWS)
    col = me // (CORES * ROWS)
    near_col = col + 1 - 2 * lax.rem(col, PAIR)
    cross_col = lax.rem(col + PAIR, cols)
    far_col = lax.rem(near_col + PAIR, cols)
    leg_cols = (far_col, cross_col, near_col, col)
    mate = seat(col, row, 1 - core)
    across = seat(col, 1 - row, core)

    barrier = pltpu.get_barrier_semaphore()

    def tell(sem, target):
        pl.semaphore_signal(
            sem, inc=1, device_id={"freq": target}, device_id_type=pl.DeviceIdType.MESH
        )

    def tell_line(sem):
        @pl.when(col > 0)
        def _():
            tell(sem, seat(col - 1, row, core))

        @pl.when(col < cols - 1)
        def _():
            tell(sem, seat(col + 1, row, core))

    beside = jnp.minimum(col, 1) + jnp.minimum(cols - 1 - col, 1)

    def at(k):
        return pl.ds(*steps[k])

    def lanes(core_at, k):
        return pl.ds(pl.multiple_of(core_at * half + steps[k][0], LANES), steps[k][1])

    def out_load(k):
        return pltpu.make_async_copy(
            x_ref.at[:, :, :, lanes(1 - core, k)], x_out.at[:, :, :, at(k)], out_sem.at[k]
        )

    def near_load(k):
        return pltpu.make_async_copy(
            x_ref.at[:, :, :, lanes(core, k)], x_near.at[:, :, :, at(k)], near_sem.at[k]
        )

    def far_copy(k):
        return remote(
            x_out.at[:, :, :, at(k)], x_far.at[:, :, :, at(k)], far_send, far_recv.at[k], mate
        )

    def green_load(k, side, part):
        core_at = core if side == 0 else 1 - core
        start, size = steps[k]
        place = CORES * 2 * start + (2 * side + part) * size
        origin = pl.multiple_of(part * CORES * half + core_at * half + start, LANES)
        return pltpu.make_async_copy(
            green_ref.at[pl.ds(origin, size), :], green_v.at[pl.ds(place, size), :], green_sem.at[k]
        )

    fi_load = pltpu.make_async_copy(fi_hbm, fi_ref, load_sem.at[0])
    map_load = pltpu.make_async_copy(map_ref, map_v, load_sem.at[1])
    src_load = pltpu.make_async_copy(src_ref, src_v, load_sem.at[2])
    fi_load.start()
    for k in range(chunks):
        out_load(k).start()
    tell(barrier, mate)
    tell(barrier, across)
    tell_line(barrier)
    for k in range(chunks):
        near_load(k).start()

    table_rows = 2 * freqs
    span = CORES * samples
    line = lax.broadcasted_iota(jnp.int32, (table_rows, span), 0)
    column = lax.broadcasted_iota(jnp.int32, (table_rows, span), 1)
    wide = span * SUBLANES
    spread = lax.broadcasted_iota(jnp.int32, (span, wide), 1) // SUBLANES == lax.broadcasted_iota(
        jnp.int32, (span, wide), 0
    )
    fi_load.wait()
    bins = jnp.zeros((table_rows, span), jnp.int32)
    for side in range(ROWS):
        for leg in range(LEGS):
            for k in range(CORES):
                to_row = 1 - row if side == 0 else row
                place = (side * LEGS + leg) * CORES + k
                bins = jnp.where(line // 2 == place, fi_ref[seat(leg_cols[leg], to_row, k)], bins)
    time = jnp.where(column < samples, me * samples + column, (mate - 1) * samples + column)
    angles = lax.rem(bins * time, length).astype(f32) * f32(2.0 * math.pi / length)
    small = jnp.where(line % 2 == 0, jnp.cos(angles), -jnp.sin(angles)).astype(bf16)
    stretched = jnp.dot(small, jnp.where(spread, 1.0, 0.0).astype(bf16), preferred_element_type=f32)
    same_shot = lax.broadcasted_iota(jnp.int32, (SUBLANES, wide), 1) % SUBLANES == (
        lax.broadcasted_iota(jnp.int32, (SUBLANES, wide), 0)
    )
    for r in range(table_rows):
        spread_row = jnp.broadcast_to(stretched[r : r + 1, :], (SUBLANES, wide))
        table[r * SUBLANES : (r + 1) * SUBLANES, :] = jnp.where(same_shot, spread_row, 0.0).astype(
            bf16
        )

    pl.semaphore_wait(barrier, 2 + beside)
    for k in range(chunks):
        out_load(k).wait()
        far_copy(k).start()
    map_load.start()
    src_load.start()
    for k in range(chunks):
        for side in range(CORES):
            for part in range(2):
                green_load(k, side, part).start()
    tell_line(line_sem.at[0])

    rows = LEGS * CORES * 2 * SUBLANES

    def partial(side, fold, k):
        size = steps[k][1]
        total = None
        for part, ref in enumerate((x_near, x_far)):
            seen = ref[:, fold, :, at(k)].reshape(depth, size)
            weights = table[side * rows : (side + 1) * rows, part * depth : (part + 1) * depth]
            term = jnp.dot(weights, seen, preferred_element_type=f32)
            total = term if total is None else total + term
        return total

    def fill(ref, side, k):
        for fold in range(folds):
            total = partial(side, fold, k)
            for leg in range(LEGS):
                for line_at in range(2 * CORES):
                    first = (leg * 2 * CORES + line_at) * SUBLANES
                    ref[leg, line_at * folds + fold, :, at(k)] = total[
                        first : first + SUBLANES
                    ].astype(ref.dtype)

    def y_copy(leg, k):
        return remote(
            y_send.at[leg, :, :, at(k)],
            y_recv.at[leg, :, :, at(k)],
            ys_sem,
            yr_sem.at[leg, k],
            across,
        )

    def pick(core_at):
        return pl.ds(core_at * groups, groups)

    def deliver(src_ref_at, kind, k, sem, arrived, to_col, to_row):
        for side in range(CORES):
            to_core = core if side == 0 else 1 - core
            remote(
                src_ref_at(to_core),
                fin.at[kind * CORES + side, :, :, at(k)],
                sem,
                arrived,
                seat(to_col, to_row, to_core),
            ).start()

    def last_copies(k):
        deliver(
            lambda c: y_send.at[LEGS - 1, pick(c), :, at(k)], 0, k, ys_sem, last_sem.at[k], col, 1 - row
        )

    def own_copy(k):
        return remote(
            own_send.at[:, :, at(k)], fin.at[3 * CORES, :, :, at(k)], os_sem, fin_sem.at[k], mate
        )

    def send_partial(k):
        near_load(k).wait()
        far_copy(k).wait_recv()
        fill(y_send, 0, k)
        y_copy(0, k).start()
        y_copy(1, k).start()

    def keep_partial(k):
        fill(y_keep, 1, k)
        own_send[:, :, at(k)] = y_keep[LEGS - 1, pick(1 - core), :, at(k)].astype(bf16)
        own_copy(k).start()

    def relay_copy(k):
        return remote(
            relay_send.at[:, :, at(k)],
            relay_recv.at[:, :, at(k)],
            rs_sem,
            rr_sem.at[k],
            seat(near_col, row, core),
        )

    def joined(leg, k):
        y_copy(leg, k).wait_recv()
        return y_keep[leg, :, :, at(k)] + y_recv[leg, :, :, at(k)].astype(f32)

    def pass_on(k):
        relay_send[:, :, at(k)] = joined(0, k).astype(bf16)
        relay_copy(k).start()

    def cross(k):
        total = joined(1, k)
        relay_copy(k).wait_recv()
        cross_send[:, :, at(k)] = (total + relay_recv[:, :, at(k)].astype(f32)).astype(bf16)
        deliver(lambda c: cross_send.at[pick(c), :, at(k)], 2, k, cs_sem, fin_sem.at[k], cross_col, row)

    def close(k):
        close_send[:, :, at(k)] = joined(2, k).astype(bf16)
        deliver(lambda c: close_send.at[pick(c), :, at(k)], 1, k, ns_sem, fin_sem.at[k], near_col, row)

    tiles = map_v.shape[1]

    def make_mask():
        map_load.wait()
        in_tile = lax.broadcasted_iota(jnp.int32, (tiles, points), 1) // (
            points // tiles
        ) == lax.broadcasted_iota(jnp.int32, (tiles, points), 0)
        mask_v[...] = jnp.dot(
            map_v[...].astype(f32).astype(bf16),
            jnp.where(in_tile, 1.0, 0.0).astype(bf16),
            preferred_element_type=f32,
        )
        acc[...] = jnp.zeros_like(acc)

    deep = CORES * half // map_v.shape[0]

    def mask_chunk(k):
        start, size = steps[k]
        whole = green_v.at[pl.ds(CORES * 2 * start, CORES * 2 * size), :]
        pltpu.make_async_copy(whole, whole, green_sem.at[k]).wait()
        for side in range(CORES):
            core_at = core if side == 0 else 1 - core
            for i in range(size // deep):
                seen = mask_v[pl.ds((core_at * half + start) // deep + i, 1), :]
                seen = jnp.broadcast_to(seen, (deep, points)).astype(bf16)
                for part in range(2):
                    place = CORES * 2 * start + (2 * side + part) * size + i * deep
                    green_v[place : place + deep, :] = green_v[place : place + deep, :] * seen

    def consume(k):
        start, size = steps[k]
        wait_fin(k)
        own = y_keep[LEGS - 1, pick(core), :, at(k)]
        sums = []
        for side in range(CORES):
            total = own if side == 0 else fin[3 * CORES, :, :, at(k)].astype(f32)
            sums.append(
                total
                + fin[CORES + side, :, :, at(k)].astype(f32)
                + fin[2 * CORES + side, :, :, at(k)].astype(f32)
            )
        wait_last(k)
        parts = []
        for side in range(CORES):
            total = sums[side] + fin[side, :, :, at(k)].astype(f32)
            spectrum = total.reshape(block, size) * f32(1.0 / math.sqrt(length))
            turned = jnp.concatenate((spectrum[block // 2 :], -spectrum[: block // 2]), axis=0)
            parts += [spectrum.astype(bf16), turned.astype(bf16)]
        acc[...] += jnp.dot(
            jnp.concatenate(parts, axis=1),
            green_v[CORES * 2 * start : CORES * 2 * (start + size), :],
            preferred_element_type=f32,
        )

    def wait_fin(k):
        five = fin.at[pl.ds(CORES, 2 * CORES + 1), :, :, at(k)]
        pltpu.make_async_copy(five, five, fin_sem.at[k]).wait()

    def wait_last(k):
        two = fin.at[pl.ds(0, CORES), :, :, at(k)]
        pltpu.make_async_copy(two, two, last_sem.at[k]).wait()

    for k in range(chunks):
        send_partial(k)
        if k == 1:
            pl.semaphore_wait(line_sem.at[0], beside)
            tell_line(line_sem.at[1])
        if k == 2:
            pl.semaphore_wait(line_sem.at[1], beside)
            tell(pair_sem, mate)
    for k in range(chunks):
        y_copy(2, k).start()
    keep_partial(0)
    pl.semaphore_wait(pair_sem, 1)
    tell(row_sem, across)
    for k in range(chunks):
        last_copies(k)
    keep_partial(1)

    events = []
    clock = 0.0
    unit = 0.7 / (2 * LANES)
    for k in range(chunks):
        clock += steps[k][1] * unit
        events.append((clock, 0, lambda k=k: pass_on(k)))
        ready = clock + 2.2 + steps[k][1] * unit
        clock += steps[k][1] * unit
        events.append((max(clock, ready), 1, lambda k=k: cross(k)))
    for k in range(chunks):
        clock += steps[k][1] * unit
        events.append((clock, 2, lambda k=k: close(k)))
    for k in range(chunks):
        clock += steps[k][1] * unit
        events.append((clock, 4, lambda k=k: consume(k)))
    for k in range(2, chunks):
        events.append((0.2 + 1.4 * (k - 2), 3, lambda k=k: keep_partial(k)))
    events.append((1.0, 5, make_mask))
    for k in range(chunks):
        events.append((3.0 + 0.9 * k, 6, lambda k=k: mask_chunk(k)))
    for _, _, run in sorted(events, key=lambda e: e[:2]):
        run()

    src_load.wait()
    product = src_v[...].astype(f32) * acc[...]
    folded = product[0:SUBLANES]
    for first in range(SUBLANES, block, SUBLANES):
        folded = folded + product[first : first + SUBLANES]
    flat = jnp.broadcast_to(jnp.sum(folded, axis=0, keepdims=True), (SUBLANES, points))
    each = points // shards
    for d in range(shards):
        i_send[d] = pltpu.roll(flat, (points - d * each) % points, 1)[0:1, :LANES]

    def i_copy(step):
        to = lax.rem(me + step, shards)
        return remote(i_send.at[to], i_recv.at[step], is_sem, ir_sem, to)

    pl.semaphore_wait(row_sem, 1)
    for step in range(1, shards):
        i_copy(step).start()
    total = i_send[me]
    others = i_recv.at[pl.ds(1, shards - 1)]
    pltpu.make_async_copy(others, others, ir_sem).wait()
    for step in range(1, shards):
        total = total + i_recv[step]
    out_ref[...] = total

    for sent, sem in (
        (x_out, far_send),
        (y_send, ys_sem),
        (relay_send, rs_sem),
        (cross_send, cs_sem),
        (close_send, ns_sem),
        (own_send, os_sem),
        (others, is_sem),
    ):
        pltpu.make_async_copy(sent, sent, sem).wait()


def fused_body(traces, freq_index, block_map, green_rec, green_src):
    shards = lax.axis_size("freq")
    samples, receivers, shots = traces.shape
    points = green_rec.shape[3]
    freqs = freq_index.shape[0]
    half = receivers // CORES
    chunks = len(chunks_of(half))
    folds = shots // SUBLANES
    records = jnp.transpose(traces, (0, 2, 1)).reshape(samples, folds, SUBLANES, receivers)
    green = green_rec.reshape(2 * receivers, points)
    sources = green_src.reshape(2 * shots, points)
    block = 2 * shots
    groups = 2 * folds
    bf16, f32 = jnp.bfloat16, jnp.float32
    dma = pltpu.SemaphoreType.DMA
    regular = pltpu.SemaphoreType.REGULAR
    outside = pl.BlockSpec(memory_space=pltpu.HBM)
    piece = (CORES * groups, SUBLANES, half)
    image = pl.pallas_call(
        imaging_kernel,
        out_shape=jax.ShapeDtypeStruct((1, LANES), f32),
        in_specs=[outside] * 5,
        out_specs=pl.BlockSpec(memory_space=pltpu.VMEM),
        scratch_shapes=[
            pltpu.SMEM(freq_index.shape, jnp.int32),
            pltpu.VMEM((samples, folds, SUBLANES, half), bf16),
            pltpu.VMEM((samples, folds, SUBLANES, half), bf16),
            pltpu.VMEM((samples, folds, SUBLANES, half), bf16),
            pltpu.VMEM((2 * freqs * SUBLANES, CORES * samples * SUBLANES), bf16),
            pltpu.VMEM((LEGS,) + piece, bf16),
            pltpu.VMEM((LEGS,) + piece, f32),
            pltpu.VMEM((LEGS - 1,) + piece, bf16),
            pltpu.VMEM(piece, bf16),
            pltpu.VMEM(piece, bf16),
            pltpu.VMEM(piece, bf16),
            pltpu.VMEM(piece, bf16),
            pltpu.VMEM((groups, SUBLANES, half), bf16),
            pltpu.VMEM((3 * CORES + 1, groups, SUBLANES, half), bf16),
            pltpu.VMEM((2 * receivers, points), bf16),
            pltpu.VMEM((block, points), bf16),
            pltpu.VMEM(block_map.shape, jnp.int32),
            pltpu.VMEM((block_map.shape[0], points), f32),
            pltpu.VMEM((block, points), f32),
            pltpu.VMEM((shards, 1, LANES), f32),
            pltpu.VMEM((shards, 1, LANES), f32),
            dma((chunks,)),
            dma((chunks,)),
            dma((3,)),
            dma((chunks,)),
            dma,
            dma((chunks,)),
            dma,
            dma((LEGS - 1, chunks)),
            dma,
            dma((chunks,)),
            dma,
            dma,
            dma,
            dma((chunks,)),
            dma((chunks,)),
            dma,
            dma,
            regular((PAIR,)),
            regular,
            regular,
        ],
        compiler_params=pltpu.CompilerParams(
            collective_id=0, has_side_effects=True, vmem_limit_bytes=48 * 1024 * 1024
        ),
    )(
        *(
            pltpu.with_memory_space_constraint(array, pltpu.HBM)
            for array in (records, freq_index, block_map, green, sources)
        )
    )
    return image[0, : points // shards]


def moves_less(traces, freq_index, block_map, green_rec):
    shards = lax.axis_size("freq")
    samples, receivers, shots = traces.shape
    freqs = freq_index.shape[0]
    return (
        2 * freqs <= samples
        and freqs == shards
        and shards == 2 * PAIR * ROWS * CORES
        and shots % SUBLANES == 0
        and receivers % (CORES * LANES) == 0
        and LANES % (receivers // block_map.shape[0]) == 0
        and green_rec.shape[3] % LANES == 0
        and green_rec.shape[3] // shards <= LANES
    )


def chosen_body(traces, freq_index, block_map, green_rec, green_src):
    fused = moves_less(traces, freq_index, block_map, green_rec)
    return (fused_body if fused else body)(traces, freq_index, block_map, green_rec, green_src)


def solution(mesh):
    in_specs = (
        P("freq", None, "groups"),
        P(),
        P(),
        P("freq", None, None, "groups"),
        P("freq", None, None, "groups"),
    )
    out_specs = P(("groups", "freq"))
    return jax.shard_map(chosen_body, mesh=mesh, in_specs=in_specs, out_specs=out_specs, check_vma=False)
```

time: 30.1 us -> 26.9 us (0.89)
  Pallas kernels: 29.4 us -> 26.2 us
    pallas_call x1, Pallas kernels: 29.4 us -> 26.2 us  [fused_body(): pl.pallas_call(imaging_kernel, out_shape=jax.ShapeDtypeStruct((1, LANES),...]
where the time goes in v1:
time: 26.9 us; the launch traced here: 26.7 us
  Pallas kernels  26.2 us (97%)
  local copies, waits for them, and re-layouts  0.51 us (2%)
    pallas_call x1, Pallas kernels, fused_body(): pl.pallas_call(imaging_kernel, out_shape=jax.ShapeDtypeStruct((1, LANES),...  26.2 us

profile of v1, /device:TPU:0, one launch (start us, length us, event | category | flops | bytes accessed | tf_op | source)
XLA Modules:
  0.0 26.7 jit_solution(18415620667720271559)
XLA Ops:
  0.0 26.2 %shard_map.55 = f32[1,128]{1,0:T(1,128)S(1)} custom-call(bf16[64,2,8,2048]{3,2,1,0:T(8,128)(2,1)} %bitcast.8, s32[16]{0:T(128)} %fi_hbm.1, s32[64,64]{1,0:T(8,128)} %map_ref.1, bf16[4096,768]{1,0:T(8,128)(2,1)} %bitcast.7, bf16[32,768]{1,0:T(8,128)(2,1)} %bitcast.9), custom_call_target="tpu_custom_call" | custom-call | tf_op jit(solution)/shard_map/pallas_call | solution.py:509
  26.2 0.5 %slice_bitcast_fusion = f32[48]{0:T(128)} fusion(f32[1,128]{1,0:T(1,128)S(1)} %shard_map.55), kind=kLoop, calls=%fused_computation | loop fusion | bytes 384 | tf_op jit(solution)/shard_map/squeeze | solution.py:566

commit v2 on v1

--- a/solution.py
+++ b/solution.py
@@ -57,11 +57,11 @@
 LANES = 128
 SUBLANES = 8
 LEGS = 4
+DIRECT = 1
 
 
 def chunks_of(half):
-    first = (LANES, LANES) if half > 2 * LANES else (LANES,) * (half // LANES)
-    sizes = list(first)
+    sizes = [LANES, LANES]
     while sum(sizes) < half:
         sizes.append(min(2 * LANES, half - sum(sizes)))
     return tuple((sum(sizes[:k]), size) for k, size in enumerate(sizes))
@@ -103,6 +103,12 @@
     close_send,
     own_send,
     fin,
+    d_send,
+    d_keep,
+    d_recv,
+    d_sum,
+    d_own,
+    d_fin,
     green_v,
     src_v,
     map_v,
@@ -125,6 +131,10 @@
     os_sem,
     fin_sem,
     last_sem,
+    ds_sem,
+    dr_sem,
+    dp_sem,
+    df_sem,
     is_sem,
     ir_sem,
     line_sem,
@@ -137,6 +147,7 @@
     length = samples * shards
     steps = chunks_of(half)
     chunks = len(steps)
+    folded = [k for k in range(chunks) if k != DIRECT]
     freqs = fi_ref.shape[0]
     points = acc.shape[1]
     block = acc.shape[0]
@@ -200,20 +211,22 @@
         place = CORES * 2 * start + (2 * side + part) * size
         origin = pl.multiple_of(part * CORES * half + core_at * half + start, LANES)
         return pltpu.make_async_copy(
-            green_ref.at[pl.ds(origin, size), :], green_v.at[pl.ds(place, size), :], green_sem.at[k]
+            green_ref.at[pl.ds(origin, size), :], green_v.at[pl.ds(place, size), :], green_sem
         )
 
     fi_load = pltpu.make_async_copy(fi_hbm, fi_ref, load_sem.at[0])
     map_load = pltpu.make_async_copy(map_ref, map_v, load_sem.at[1])
     src_load = pltpu.make_async_copy(src_ref, src_v, load_sem.at[2])
     fi_load.start()
-    for k in range(chunks):
-        out_load(k).start()
+    order = folded[:2] + [DIRECT] + folded[2:]
+    out_load(order[0]).start()
+    for k, later in zip(order, order[1:]):
+        out_load(later).start()
+        near_load(k).start()
+    near_load(order[-1]).start()
     tell(barrier, mate)
     tell(barrier, across)
     tell_line(barrier)
-    for k in range(chunks):
-        near_load(k).start()
 
     table_rows = 2 * freqs
     span = CORES * samples
@@ -223,6 +236,9 @@
     spread = lax.broadcasted_iota(jnp.int32, (span, wide), 1) // SUBLANES == lax.broadcasted_iota(
         jnp.int32, (span, wide), 0
     )
+    pl.semaphore_wait(barrier, 2 + beside)
+    out_load(order[0]).wait()
+    far_copy(order[0]).start()
     fi_load.wait()
     bins = jnp.zeros((table_rows, span), jnp.int32)
     for side in range(ROWS):
@@ -244,17 +260,21 @@
             bf16
         )
 
-    pl.semaphore_wait(barrier, 2 + beside)
-    for k in range(chunks):
+    tell_line(line_sem.at[0])
+
+    def hand_over(k):
         out_load(k).wait()
         far_copy(k).start()
+
+    hand_over(order[1])
+    hand_over(order[2])
     map_load.start()
     src_load.start()
-    for k in range(chunks):
+
+    def start_green(k):
         for side in range(CORES):
             for part in range(2):
                 green_load(k, side, part).start()
-    tell_line(line_sem.at[0])
 
     rows = LEGS * CORES * 2 * SUBLANES
 
@@ -316,7 +336,6 @@
         far_copy(k).wait_recv()
         fill(y_send, 0, k)
         y_copy(0, k).start()
-        y_copy(1, k).start()
 
     def keep_partial(k):
         fill(y_keep, 1, k)
@@ -350,10 +369,55 @@
         close_send[:, :, at(k)] = joined(2, k).astype(bf16)
         deliver(lambda c: close_send.at[pick(c), :, at(k)], 1, k, ns_sem, fin_sem.at[k], near_col, row)
 
+    def direct_copy(leg):
+        return remote(
+            d_send.at[leg], d_recv.at[leg], ds_sem, dr_sem, seat(leg_cols[leg], row, core)
+        )
+
+    def send_direct():
+        near_load(DIRECT).wait()
+        far_copy(DIRECT).wait_recv()
+        for side in range(ROWS):
+            for fold in range(folds):
+                total = partial(side, fold, DIRECT)
+                for leg in range(LEGS):
+                    for line_at in range(2 * CORES):
+                        first = (leg * 2 * CORES + line_at) * SUBLANES
+                        place = (side * 2 * CORES + line_at) * folds + fold
+                        value = total[first : first + SUBLANES]
+                        if leg < LEGS - 1:
+                            d_send[leg, place] = value.astype(bf16)
+                        else:
+                            d_keep[place] = value
+        for leg in range(LEGS - 1):
+            direct_copy(leg).start()
+
+    def join_direct():
+        pltpu.make_async_copy(d_recv, d_recv, dr_sem).wait()
+        total = d_keep[...]
+        for leg in range(LEGS - 1):
+            total = total + d_recv[leg].astype(f32)
+        d_keep[...] = total
+        d_sum[...] = total.astype(bf16)
+        d_own[...] = d_keep[pl.ds((CORES + core) * groups, groups)]
+        for slot, side, to_core, target in (
+            (1, 0, core, across),
+            (2, 0, 1 - core, seat(col, 1 - row, 1 - core)),
+            (0, 1, 1 - core, mate),
+        ):
+            remote(
+                d_sum.at[pl.ds((side * CORES + to_core) * groups, groups)],
+                d_fin.at[slot],
+                dp_sem,
+                df_sem,
+                target,
+            ).start()
+
     tiles = map_v.shape[1]
 
     def make_mask():
         map_load.wait()
+        pltpu.make_async_copy(green_v, green_v, green_sem).wait()
         in_tile = lax.broadcasted_iota(jnp.int32, (tiles, points), 1) // (
             points // tiles
         ) == lax.broadcasted_iota(jnp.int32, (tiles, points), 0)
@@ -368,8 +432,6 @@
 
     def mask_chunk(k):
         start, size = steps[k]
-        whole = green_v.at[pl.ds(CORES * 2 * start, CORES * 2 * size), :]
-        pltpu.make_async_copy(whole, whole, green_sem.at[k]).wait()
         for side in range(CORES):
             core_at = core if side == 0 else 1 - core
             for i in range(size // deep):
@@ -379,8 +441,20 @@
                     place = CORES * 2 * start + (2 * side + part) * size + i * deep
                     green_v[place : place + deep, :] = green_v[place : place + deep, :] * seen
 
+    def use(k, totals):
+        start, size = steps[k]
+        parts = []
+        for total in totals:
+            spectrum = total.reshape(block, size) * f32(1.0 / math.sqrt(length))
+            turned = jnp.concatenate((spectrum[block // 2 :], -spectrum[: block // 2]), axis=0)
+            parts += [spectrum.astype(bf16), turned.astype(bf16)]
+        acc[...] += jnp.dot(
+            jnp.concatenate(parts, axis=1),
+            green_v[CORES * 2 * start : CORES * 2 * (start + size), :],
+            preferred_element_type=f32,
+        )
+
     def consume(k):
-        start, size = steps[k]
         wait_fin(k)
         own = y_keep[LEGS - 1, pick(core), :, at(k)]
         sums = []
@@ -392,16 +466,16 @@
                 + fin[2 * CORES + side, :, :, at(k)].astype(f32)
             )
         wait_last(k)
-        parts = []
-        for side in range(CORES):
-            total = sums[side] + fin[side, :, :, at(k)].astype(f32)
-            spectrum = total.reshape(block, size) * f32(1.0 / math.sqrt(length))
-            turned = jnp.concatenate((spectrum[block // 2 :], -spectrum[: block // 2]), axis=0)
-            parts += [spectrum.astype(bf16), turned.astype(bf16)]
-        acc[...] += jnp.dot(
-            jnp.concatenate(parts, axis=1),
-            green_v[CORES * 2 * start : CORES * 2 * (start + size), :],
-            preferred_element_type=f32,
+        use(k, [sums[side] + fin[side, :, :, at(k)].astype(f32) for side in range(CORES)])
+
+    def consume_direct():
+        pltpu.make_async_copy(d_fin, d_fin, df_sem).wait()
+        use(
+            DIRECT,
+            [
+                d_own[...] + d_fin[1].astype(f32),
+                d_fin[0].astype(f32) + d_fin[2].astype(f32),
+            ],
         )
 
     def wait_fin(k):
@@ -412,43 +486,59 @@
         two = fin.at[pl.ds(0, CORES), :, :, at(k)]
         pltpu.make_async_copy(two, two, last_sem.at[k]).wait()
 
+    send_partial(order[0])
+    hand_over(order[3])
+    pl.semaphore_wait(line_sem.at[0], beside)
+    tell_line(line_sem.at[1])
+    send_partial(order[1])
+    for k in order[4:]:
+        hand_over(k)
+    pl.semaphore_wait(line_sem.at[1], beside)
+    tell(pair_sem, mate)
     for k in range(chunks):
+        start_green(k)
+    send_direct()
+    for at_fold, k in enumerate(folded[2:]):
         send_partial(k)
-        if k == 1:
-            pl.semaphore_wait(line_sem.at[0], beside)
-            tell_line(line_sem.at[1])
-        if k == 2:
-            pl.semaphore_wait(line_sem.at[1], beside)
-            tell(pair_sem, mate)
-    for k in range(chunks):
-        y_copy(2, k).start()
-    keep_partial(0)
+        keep_partial(folded[at_fold])
+    for leg in (1, 2):
+        for k in folded:
+            y_copy(leg, k).start()
     pl.semaphore_wait(pair_sem, 1)
     tell(row_sem, across)
+
+    def send_last():
+        join_direct()
+        for k in folded:
+            last_copies(k)
+
+    wire = 0.7 / (2 * LANES)
+    hop = 2.6
+    events = [(4.0, 5, make_mask), (4.3, 7, send_last)]
+    for place, k in enumerate(folded[len(folded) - 2 :]):
+        events.append((0.8 + 0.7 * place, 8, lambda k=k: keep_partial(k)))
+    clock = mid = 0.0
+    handed = {}
+    for leg in range(LEGS):
+        for k in folded:
+            span = steps[k][1] * wire
+            clock += span
+            if leg == 0:
+                events.append((clock, leg, lambda k=k: pass_on(k)))
+                handed[k] = clock + span + hop
+            elif leg == 1:
+                ready = max(clock, handed[k])
+                mid = max(mid, ready) + 2 * span
+                handed[k] = mid + hop + 0.5
+                events.append((ready, leg, lambda k=k: cross(k)))
+            elif leg == 2:
+                handed[k] = max(handed[k], clock + span + hop)
+                events.append((clock, leg, lambda k=k: close(k)))
+            else:
+                events.append((max(clock, handed[k]), leg, lambda k=k: consume(k)))
+    events.append((8.6, 9, consume_direct))
     for k in range(chunks):
-        last_copies(k)
-    keep_partial(1)
-
-    events = []
-    clock = 0.0
-    unit = 0.7 / (2 * LANES)
-    for k in range(chunks):
-        clock += steps[k][1] * unit
-        events.append((clock, 0, lambda k=k: pass_on(k)))
-        ready = clock + 2.2 + steps[k][1] * unit
-        clock += steps[k][1] * unit
-        events.append((max(clock, ready), 1, lambda k=k: cross(k)))
-    for k in range(chunks):
-        clock += steps[k][1] * unit
-        events.append((clock, 2, lambda k=k: close(k)))
-    for k in range(chunks):
-        clock += steps[k][1] * unit
-        events.append((clock, 4, lambda k=k: consume(k)))
-    for k in range(2, chunks):
-        events.append((0.2 + 1.4 * (k - 2), 3, lambda k=k: keep_partial(k)))
-    events.append((1.0, 5, make_mask))
-    for k in range(chunks):
-        events.append((3.0 + 0.9 * k, 6, lambda k=k: mask_chunk(k)))
+        events.append((5.0 + 0.6 * k, 6, lambda k=k: mask_chunk(k)))
     for _, _, run in sorted(events, key=lambda e: e[:2]):
         run()
 
@@ -471,21 +561,23 @@
         i_copy(step).start()
     total = i_send[me]
     others = i_recv.at[pl.ds(1, shards - 1)]
+    rest = pl.ds(0, half - steps[DIRECT][1])
+    for sent, sem in (
+        (x_out, far_send),
+        (y_send.at[:, :, :, rest], ys_sem),
+        (relay_send.at[:, :, rest], rs_sem),
+        (cross_send.at[:, :, rest], cs_sem),
+        (close_send.at[:, :, rest], ns_sem),
+        (own_send.at[:, :, rest], os_sem),
+        (d_send, ds_sem),
+        (d_fin, dp_sem),
+    ):
+        pltpu.make_async_copy(sent, sent, sem).wait()
     pltpu.make_async_copy(others, others, ir_sem).wait()
     for step in range(1, shards):
         total = total + i_recv[step]
     out_ref[...] = total
-
-    for sent, sem in (
-        (x_out, far_send),
-        (y_send, ys_sem),
-        (relay_send, rs_sem),
-        (cross_send, cs_sem),
-        (close_send, ns_sem),
-        (own_send, os_sem),
-        (others, is_sem),
-    ):
-        pltpu.make_async_copy(sent, sent, sem).wait()
+    pltpu.make_async_copy(others, others, is_sem).wait()
 
 
 def fused_body(traces, freq_index, block_map, green_rec, green_src):
@@ -506,6 +598,7 @@
     regular = pltpu.SemaphoreType.REGULAR
     outside = pl.BlockSpec(memory_space=pltpu.HBM)
     piece = (CORES * groups, SUBLANES, half)
+    direct = (ROWS * CORES * groups, SUBLANES, chunks_of(half)[DIRECT][1])
     image = pl.pallas_call(
         imaging_kernel,
         out_shape=jax.ShapeDtypeStruct((1, LANES), f32),
@@ -526,6 +619,12 @@
             pltpu.VMEM(piece, bf16),
             pltpu.VMEM((groups, SUBLANES, half), bf16),
             pltpu.VMEM((3 * CORES + 1, groups, SUBLANES, half), bf16),
+            pltpu.VMEM((LEGS - 1,) + direct, bf16),
+            pltpu.VMEM(direct, f32),
+            pltpu.VMEM((LEGS - 1,) + direct, bf16),
+            pltpu.VMEM(direct, bf16),
+            pltpu.VMEM((groups,) + direct[1:], f32),
+            pltpu.VMEM((ROWS * CORES - 1, groups) + direct[1:], bf16),
             pltpu.VMEM((2 * receivers, points), bf16),
             pltpu.VMEM((block, points), bf16),
             pltpu.VMEM(block_map.shape, jnp.int32),
@@ -536,7 +635,7 @@
             dma((chunks,)),
             dma((chunks,)),
             dma((3,)),
-            dma((chunks,)),
+            dma,
             dma,
             dma((chunks,)),
             dma,
@@ -548,6 +647,10 @@
             dma,
             dma((chunks,)),
             dma((chunks,)),
+            dma,
+            dma,
+            dma,
+            dma,
             dma,
             dma,
             regular((PAIR,)),
@@ -576,6 +679,7 @@
         and shards == 2 * PAIR * ROWS * CORES
         and shots % SUBLANES == 0
         and receivers % (CORES * LANES) == 0
+        and receivers >= CORES * 5 * LANES
         and LANES % (receivers // block_map.shape[0]) == 0
         and green_rec.shape[3] % LANES == 0
         and green_rec.shape[3] // shards <= LANES

time: 26.9 us -> 25.8 us (0.959)
  Pallas kernels: 26.2 us -> 25.2 us
    pallas_call x1, Pallas kernels: 26.2 us -> 25.2 us  [fused_body(): pl.pallas_call(imaging_kernel, out_shape=jax.ShapeDtypeStruct((1, LANES),...]
where the time goes in v2:
time: 25.8 us; the launch traced here: 25.7 us
  Pallas kernels  25.2 us (98%)
  local copies, waits for them, and re-layouts  0.51 us (2%)
    pallas_call x1, Pallas kernels, fused_body(): pl.pallas_call(imaging_kernel, out_shape=jax.ShapeDtypeStruct((1, LANES),...  25.2 us

profile of v2, /device:TPU:0, one launch (start us, length us, event | category | flops | bytes accessed | tf_op | source)
XLA Modules:
  0.0 25.7 jit_solution(10720073929412176018)
XLA Ops:
  0.0 25.2 %shard_map.55 = f32[1,128]{1,0:T(1,128)S(1)} custom-call(bf16[64,2,8,2048]{3,2,1,0:T(8,128)(2,1)} %bitcast.8, s32[16]{0:T(128)} %fi_hbm.1, s32[64,64]{1,0:T(8,128)} %map_ref.1, bf16[4096,768]{1,0:T(8,128)(2,1)} %bitcast.7, bf16[32,768]{1,0:T(8,128)(2,1)} %bitcast.9), custom_call_target="tpu_custom_call" | custom-call | tf_op jit(solution)/shard_map/pallas_call | solution.py:602
  25.2 0.5 %slice_bitcast_fusion = f32[48]{0:T(128)} fusion(f32[1,128]{1,0:T(1,128)S(1)} %shard_map.55), kind=kLoop, calls=%fused_computation | loop fusion | bytes 384 | tf_op jit(solution)/shard_map/squeeze | solution.py:669

commit v3 on v2

--- a/solution.py
+++ b/solution.py
@@ -1,3 +1,4 @@
+import functools
 import math
 
 import jax
@@ -58,13 +59,28 @@
 SUBLANES = 8
 LEGS = 4
 DIRECT = 1
-
-
-def chunks_of(half):
+WIDE = 2 * LANES
+PIECE = LANES
+AHEAD = 2
+MIXED = True
+MASK = 3.6
+LATE = -0.1
+
+
+def groups_of(half):
     sizes = [LANES, LANES]
     while sum(sizes) < half:
-        sizes.append(min(2 * LANES, half - sum(sizes)))
+        sizes.append(min(WIDE, half - sum(sizes)))
     return tuple((sum(sizes[:k]), size) for k, size in enumerate(sizes))
+
+
+def pieces_of(group):
+    start, size = group
+    return tuple((lane, min(PIECE, start + size - lane)) for lane in range(start, start + size, PIECE))
+
+
+def chunks_of(half):
+    return tuple(piece for group in groups_of(half) for piece in pieces_of(group))
 
 
 def seat(col, row, core):
@@ -82,7 +98,38 @@
     )
 
 
-def imaging_kernel(
+def imaging_kernel(*refs):
+    half = refs[9].shape[0] * LANES
+    chunks = len(chunks_of(half))
+    packs = len(groups_of(half))
+    dma = pltpu.SemaphoreType.DMA
+    pl.run_scoped(
+        functools.partial(imaging, *refs),
+        dma((packs,)),
+        dma((packs,)),
+        dma((3,)),
+        dma,
+        dma,
+        dma((packs,)),
+        dma,
+        dma((LEGS - 1, chunks)),
+        dma,
+        dma((chunks,)),
+        dma,
+        dma,
+        dma,
+        dma((chunks,)),
+        dma((chunks,)),
+        dma,
+        dma,
+        dma,
+        dma,
+        dma,
+        dma,
+    )
+
+
+def imaging(
     x_ref,
     fi_hbm,
     map_ref,
@@ -114,8 +161,11 @@
     map_v,
     mask_v,
     acc,
-    i_send,
+    flat,
     i_recv,
+    line_sem,
+    pair_sem,
+    row_sem,
     out_sem,
     near_sem,
     load_sem,
@@ -137,17 +187,18 @@
     df_sem,
     is_sem,
     ir_sem,
-    line_sem,
-    pair_sem,
-    row_sem,
 ):
-    shards = i_send.shape[0]
+    shards = i_recv.shape[0]
     cols = shards // (ROWS * CORES)
-    samples, folds, _, half = x_far.shape
+    blocks, folds, samples = x_far.shape[:3]
+    half = blocks * LANES
     length = samples * shards
     steps = chunks_of(half)
     chunks = len(steps)
-    folded = [k for k in range(chunks) if k != DIRECT]
+    packs = groups_of(half)
+    members = [[k for k in range(chunks) if p <= steps[k][0] < p + n] for p, n in packs]
+    folded = [g for g in range(len(packs)) if g != DIRECT]
+    order = folded[:AHEAD] + [DIRECT] + folded[AHEAD:]
     freqs = fi_ref.shape[0]
     points = acc.shape[1]
     block = acc.shape[0]
@@ -190,24 +241,30 @@
     def lanes(core_at, k):
         return pl.ds(pl.multiple_of(core_at * half + steps[k][0], LANES), steps[k][1])
 
-    def out_load(k):
-        return pltpu.make_async_copy(
-            x_ref.at[:, :, :, lanes(1 - core, k)], x_out.at[:, :, :, at(k)], out_sem.at[k]
-        )
-
-    def near_load(k):
-        return pltpu.make_async_copy(
-            x_ref.at[:, :, :, lanes(core, k)], x_near.at[:, :, :, at(k)], near_sem.at[k]
-        )
+    def blocks_of(k):
+        return pl.ds(packs[k][0] // LANES, packs[k][1] // LANES)
+
+    def x_load(core_at, ref, sem, k):
+        start, size = packs[k]
+        for lane in range(start, start + size, LANES):
+            origin = pl.ds(pl.multiple_of(core_at * half + lane, LANES), LANES)
+            for fold in range(folds):
+                pltpu.make_async_copy(
+                    x_ref.at[:, fold, :, origin], ref.at[lane // LANES, fold], sem.at[k]
+                ).start()
+
+    def x_wait(ref, sem, k):
+        whole = ref.at[blocks_of(k)]
+        pltpu.make_async_copy(whole, whole, sem.at[k]).wait()
 
     def far_copy(k):
         return remote(
-            x_out.at[:, :, :, at(k)], x_far.at[:, :, :, at(k)], far_send, far_recv.at[k], mate
+            x_out.at[blocks_of(k)], x_far.at[blocks_of(k)], far_send, far_recv.at[k], mate
         )
 
     def green_load(k, side, part):
         core_at = core if side == 0 else 1 - core
-        start, size = steps[k]
+        start, size = packs[k]
         place = CORES * 2 * start + (2 * side + part) * size
         origin = pl.multiple_of(part * CORES * half + core_at * half + start, LANES)
         return pltpu.make_async_copy(
@@ -217,16 +274,15 @@
     fi_load = pltpu.make_async_copy(fi_hbm, fi_ref, load_sem.at[0])
     map_load = pltpu.make_async_copy(map_ref, map_v, load_sem.at[1])
     src_load = pltpu.make_async_copy(src_ref, src_v, load_sem.at[2])
-    fi_load.start()
-    order = folded[:2] + [DIRECT] + folded[2:]
-    out_load(order[0]).start()
-    for k, later in zip(order, order[1:]):
-        out_load(later).start()
-        near_load(k).start()
-    near_load(order[-1]).start()
     tell(barrier, mate)
     tell(barrier, across)
+    x_load(1 - core, x_out, out_sem, order[0])
+    fi_load.start()
     tell_line(barrier)
+    for k, later in zip(order, order[1:]):
+        x_load(1 - core, x_out, out_sem, later)
+        x_load(core, x_near, near_sem, k)
+    x_load(core, x_near, near_sem, order[-1])
 
     table_rows = 2 * freqs
     span = CORES * samples
@@ -237,7 +293,7 @@
         jnp.int32, (span, wide), 0
     )
     pl.semaphore_wait(barrier, 2 + beside)
-    out_load(order[0]).wait()
+    x_wait(x_out, out_sem, order[0])
     far_copy(order[0]).start()
     fi_load.wait()
     bins = jnp.zeros((table_rows, span), jnp.int32)
@@ -263,11 +319,10 @@
     tell_line(line_sem.at[0])
 
     def hand_over(k):
-        out_load(k).wait()
+        x_wait(x_out, out_sem, k)
         far_copy(k).start()
 
     hand_over(order[1])
-    hand_over(order[2])
     map_load.start()
     src_load.start()
 
@@ -279,10 +334,13 @@
     rows = LEGS * CORES * 2 * SUBLANES
 
     def partial(side, fold, k):
-        size = steps[k][1]
+        start, size = packs[k]
         total = None
         for part, ref in enumerate((x_near, x_far)):
-            seen = ref[:, fold, :, at(k)].reshape(depth, size)
+            seen = jnp.concatenate(
+                [ref[start // LANES + n, fold].reshape(depth, LANES) for n in range(size // LANES)],
+                axis=1,
+            )
             weights = table[side * rows : (side + 1) * rows, part * depth : (part + 1) * depth]
             term = jnp.dot(weights, seen, preferred_element_type=f32)
             total = term if total is None else total + term
@@ -294,7 +352,7 @@
             for leg in range(LEGS):
                 for line_at in range(2 * CORES):
                     first = (leg * 2 * CORES + line_at) * SUBLANES
-                    ref[leg, line_at * folds + fold, :, at(k)] = total[
+                    ref[leg, line_at * folds + fold, :, pl.ds(*packs[k])] = total[
                         first : first + SUBLANES
                     ].astype(ref.dtype)
 
@@ -332,15 +390,16 @@
         )
 
     def send_partial(k):
-        near_load(k).wait()
+        x_wait(x_near, near_sem, k)
         far_copy(k).wait_recv()
         fill(y_send, 0, k)
-        y_copy(0, k).start()
 
     def keep_partial(k):
         fill(y_keep, 1, k)
-        own_send[:, :, at(k)] = y_keep[LEGS - 1, pick(1 - core), :, at(k)].astype(bf16)
-        own_copy(k).start()
+        lane = pl.ds(*packs[k])
+        own_send[:, :, lane] = y_keep[LEGS - 1, pick(1 - core), :, lane].astype(bf16)
+        for m in members[k]:
+            own_copy(m).start()
 
     def relay_copy(k):
         return remote(
@@ -375,7 +434,7 @@
         )
 
     def send_direct():
-        near_load(DIRECT).wait()
+        x_wait(x_near, near_sem, DIRECT)
         far_copy(DIRECT).wait_recv()
         for side in range(ROWS):
             for fold in range(folds):
@@ -431,7 +490,7 @@
     deep = CORES * half // map_v.shape[0]
 
     def mask_chunk(k):
-        start, size = steps[k]
+        start, size = packs[k]
         for side in range(CORES):
             core_at = core if side == 0 else 1 - core
             for i in range(size // deep):
@@ -442,7 +501,7 @@
                     green_v[place : place + deep, :] = green_v[place : place + deep, :] * seen
 
     def use(k, totals):
-        start, size = steps[k]
+        start, size = packs[k]
         parts = []
         for total in totals:
             spectrum = total.reshape(block, size) * f32(1.0 / math.sqrt(length))
@@ -454,19 +513,22 @@
             preferred_element_type=f32,
         )
 
-    def consume(k):
-        wait_fin(k)
-        own = y_keep[LEGS - 1, pick(core), :, at(k)]
+    def consume(g):
+        lane = pl.ds(*packs[g])
+        for k in members[g]:
+            wait_fin(k)
+        own = y_keep[LEGS - 1, pick(core), :, lane]
         sums = []
         for side in range(CORES):
-            total = own if side == 0 else fin[3 * CORES, :, :, at(k)].astype(f32)
+            total = own if side == 0 else fin[3 * CORES, :, :, lane].astype(f32)
             sums.append(
                 total
-                + fin[CORES + side, :, :, at(k)].astype(f32)
-                + fin[2 * CORES + side, :, :, at(k)].astype(f32)
+                + fin[CORES + side, :, :, lane].astype(f32)
+                + fin[2 * CORES + side, :, :, lane].astype(f32)
             )
-        wait_last(k)
-        use(k, [sums[side] + fin[side, :, :, at(k)].astype(f32) for side in range(CORES)])
+        for k in members[g]:
+            wait_last(k)
+        use(g, [sums[side] + fin[side, :, :, lane].astype(f32) for side in range(CORES)])
 
     def consume_direct():
         pltpu.make_async_copy(d_fin, d_fin, df_sem).wait()
@@ -486,82 +548,117 @@
         two = fin.at[pl.ds(0, CORES), :, :, at(k)]
         pltpu.make_async_copy(two, two, last_sem.at[k]).wait()
 
-    send_partial(order[0])
-    hand_over(order[3])
-    pl.semaphore_wait(line_sem.at[0], beside)
-    tell_line(line_sem.at[1])
-    send_partial(order[1])
-    for k in order[4:]:
-        hand_over(k)
-    pl.semaphore_wait(line_sem.at[1], beside)
-    tell(pair_sem, mate)
-    for k in range(chunks):
-        start_green(k)
-    send_direct()
-    for at_fold, k in enumerate(folded[2:]):
-        send_partial(k)
-        keep_partial(folded[at_fold])
-    for leg in (1, 2):
-        for k in folded:
-            y_copy(leg, k).start()
+    wire = 0.7 / (2 * LANES)
+    hop = 2.6
+    clock = 0.0
+    arrival = {}
+
+    def expect(leg, k):
+        nonlocal clock
+        clock += steps[k][1] * wire
+        arrival[leg, k] = clock
+
+    def start_y(leg, ks):
+        for k in ks:
+            expect(leg, k)
+            if leg < LEGS - 1:
+                y_copy(leg, k).start()
+            else:
+                last_copies(k)
+
+    def flat_of(groups_at):
+        return [k for g in groups_at for k in members[g]]
+
+    kept = 0
+    for place, g in enumerate(order):
+        if place + 2 < len(order):
+            hand_over(order[place + 2])
+        if g == DIRECT:
+            pl.semaphore_wait(line_sem.at[1], beside)
+            tell(pair_sem, mate)
+            send_direct()
+            continue
+        send_partial(g)
+        start_y(0, members[g])
+        if g == folded[0]:
+            start_y(1, members[g])
+            clock = max(clock, 0.85)
+            pl.semaphore_wait(line_sem.at[0], beside)
+            tell_line(line_sem.at[1])
+        elif place > 1:
+            keep_partial(folded[kept])
+            kept += 1
+    for g in range(len(packs)):
+        start_green(g)
+    turns = [(1, k) for k in flat_of(folded[1:])]
+    others = [(2, k) for k in flat_of(folded)]
+    if MIXED:
+        turns = [t for pair in zip(turns, others) for t in pair] + others[len(turns) :]
+    else:
+        turns += others
+    for leg, k in turns:
+        start_y(leg, [k])
+    tail = flat_of(folded[-1:])
     pl.semaphore_wait(pair_sem, 1)
     tell(row_sem, across)
+    start_y(LEGS - 1, flat_of(folded[:-1]))
 
     def send_last():
         join_direct()
-        for k in folded:
+        for k in tail:
             last_copies(k)
 
-    wire = 0.7 / (2 * LANES)
-    hop = 2.6
-    events = [(4.0, 5, make_mask), (4.3, 7, send_last)]
-    for place, k in enumerate(folded[len(folded) - 2 :]):
-        events.append((0.8 + 0.7 * place, 8, lambda k=k: keep_partial(k)))
-    clock = mid = 0.0
-    handed = {}
-    for leg in range(LEGS):
-        for k in folded:
+    for k in tail:
+        expect(LEGS - 1, k)
+    events = [(6.2, 7, send_last), (MASK, 5, make_mask)]
+    for place, g in enumerate(folded[kept:]):
+        events.append((max(arrival[0, members[g][0]] - 0.6, 0.4), 8, lambda g=g: keep_partial(g)))
+    mid = 0.0
+    for g in folded:
+        done = 0.0
+        for k in members[g]:
             span = steps[k][1] * wire
-            clock += span
-            if leg == 0:
-                events.append((clock, leg, lambda k=k: pass_on(k)))
-                handed[k] = clock + span + hop
-            elif leg == 1:
-                ready = max(clock, handed[k])
-                mid = max(mid, ready) + 2 * span
-                handed[k] = mid + hop + 0.5
-                events.append((ready, leg, lambda k=k: cross(k)))
-            elif leg == 2:
-                handed[k] = max(handed[k], clock + span + hop)
-                events.append((clock, leg, lambda k=k: close(k)))
-            else:
-                events.append((max(clock, handed[k]), leg, lambda k=k: consume(k)))
-    events.append((8.6, 9, consume_direct))
-    for k in range(chunks):
-        events.append((5.0 + 0.6 * k, 6, lambda k=k: mask_chunk(k)))
+            events.append((arrival[0, k], 0, lambda k=k: pass_on(k)))
+            merged = max(arrival[1, k], arrival[0, k] + span + hop)
+            events.append((merged, 1, lambda k=k: cross(k)))
+            mid = max(mid, merged) + 2 * span
+            events.append((arrival[2, k], 2, lambda k=k: close(k)))
+            done = max(mid + hop + 0.5, arrival[2, k] + span + hop, arrival[LEGS - 1, k], done)
+        events.append((done, 4, lambda g=g: consume(g)))
+    events.append((done + LATE, 9, consume_direct))
+    for g in range(len(packs)):
+        events.append((MASK + 0.4 + 0.6 * g, 6, lambda g=g: mask_chunk(g)))
     for _, _, run in sorted(events, key=lambda e: e[:2]):
         run()
 
     src_load.wait()
     product = src_v[...].astype(f32) * acc[...]
-    folded = product[0:SUBLANES]
+    stacked = product[0:SUBLANES]
     for first in range(SUBLANES, block, SUBLANES):
-        folded = folded + product[first : first + SUBLANES]
-    flat = jnp.broadcast_to(jnp.sum(folded, axis=0, keepdims=True), (SUBLANES, points))
+        stacked = stacked + product[first : first + SUBLANES]
+    flat[...] = jnp.sum(stacked, axis=0, keepdims=True)
     each = points // shards
-    for d in range(shards):
-        i_send[d] = pltpu.roll(flat, (points - d * each) % points, 1)[0:1, :LANES]
-
-    def i_copy(step):
-        to = lax.rem(me + step, shards)
-        return remote(i_send.at[to], i_recv.at[step], is_sem, ir_sem, to)
+
+    def window(d):
+        first = jnp.minimum(d * each // LANES, points // LANES - 2)
+        return pl.ds(pl.multiple_of(first * LANES, LANES), 2 * LANES)
+
+    peers = []
+    for leg_col in leg_cols:
+        for to_row in (1 - row, row):
+            for to_core in (1 - core, core):
+                peers.append(seat(leg_col, to_row, to_core))
+
+    def i_copy(slot):
+        to = peers[slot]
+        return remote(flat.at[:, window(to)], i_recv.at[slot], is_sem, ir_sem, to)
 
     pl.semaphore_wait(row_sem, 1)
-    for step in range(1, shards):
-        i_copy(step).start()
-    total = i_send[me]
-    others = i_recv.at[pl.ds(1, shards - 1)]
-    rest = pl.ds(0, half - steps[DIRECT][1])
+    for slot in range(shards - 1):
+        i_copy(slot).start()
+    total = flat[:, window(me)]
+    others = i_recv.at[pl.ds(0, shards - 1)]
+    rest = pl.ds(0, half - packs[DIRECT][1])
     for sent, sem in (
         (x_out, far_send),
         (y_send.at[:, :, :, rest], ys_sem),
@@ -574,9 +671,12 @@
     ):
         pltpu.make_async_copy(sent, sent, sem).wait()
     pltpu.make_async_copy(others, others, ir_sem).wait()
-    for step in range(1, shards):
-        total = total + i_recv[step]
-    out_ref[...] = total
+    for slot in range(shards - 1):
+        total = total + i_recv[slot]
+    first = jnp.minimum(me * each // LANES, points // LANES - 2) * LANES
+    total = jnp.broadcast_to(total, (SUBLANES, 2 * LANES))
+    shift = lax.rem(2 * LANES - (me * each - first), 2 * LANES)
+    out_ref[...] = pltpu.roll(total, shift, 1)[0:1, :LANES]
     pltpu.make_async_copy(others, others, is_sem).wait()
 
 
@@ -594,11 +694,10 @@
     block = 2 * shots
     groups = 2 * folds
     bf16, f32 = jnp.bfloat16, jnp.float32
-    dma = pltpu.SemaphoreType.DMA
     regular = pltpu.SemaphoreType.REGULAR
     outside = pl.BlockSpec(memory_space=pltpu.HBM)
     piece = (CORES * groups, SUBLANES, half)
-    direct = (ROWS * CORES * groups, SUBLANES, chunks_of(half)[DIRECT][1])
+    direct = (ROWS * CORES * groups, SUBLANES, groups_of(half)[DIRECT][1])
     image = pl.pallas_call(
         imaging_kernel,
         out_shape=jax.ShapeDtypeStruct((1, LANES), f32),
@@ -606,9 +705,9 @@
         out_specs=pl.BlockSpec(memory_space=pltpu.VMEM),
         scratch_shapes=[
             pltpu.SMEM(freq_index.shape, jnp.int32),
-            pltpu.VMEM((samples, folds, SUBLANES, half), bf16),
-            pltpu.VMEM((samples, folds, SUBLANES, half), bf16),
-            pltpu.VMEM((samples, folds, SUBLANES, half), bf16),
+            pltpu.VMEM((half // LANES, folds, samples, SUBLANES, LANES), bf16),
+            pltpu.VMEM((half // LANES, folds, samples, SUBLANES, LANES), bf16),
+            pltpu.VMEM((half // LANES, folds, samples, SUBLANES, LANES), bf16),
             pltpu.VMEM((2 * freqs * SUBLANES, CORES * samples * SUBLANES), bf16),
             pltpu.VMEM((LEGS,) + piece, bf16),
             pltpu.VMEM((LEGS,) + piece, f32),
@@ -630,29 +729,8 @@
             pltpu.VMEM(block_map.shape, jnp.int32),
             pltpu.VMEM((block_map.shape[0], points), f32),
             pltpu.VMEM((block, points), f32),
-            pltpu.VMEM((shards, 1, LANES), f32),
-            pltpu.VMEM((shards, 1, LANES), f32),
-            dma((chunks,)),
-            dma((chunks,)),
-            dma((3,)),
-            dma,
-            dma,
-            dma((chunks,)),
-            dma,
-            dma((LEGS - 1, chunks)),
-            dma,
-            dma((chunks,)),
-            dma,
-            dma,
-            dma,
-            dma((chunks,)),
-            dma((chunks,)),
-            dma,
-            dma,
-            dma,
-            dma,
-            dma,
-            dma,
+            pltpu.VMEM((1, points), f32),
+            pltpu.VMEM((shards, 1, 2 * LANES), f32),
             regular((PAIR,)),
             regular,
             regular,
@@ -682,6 +760,7 @@
         and receivers >= CORES * 5 * LANES
         and LANES % (receivers // block_map.shape[0]) == 0
         and green_rec.shape[3] % LANES == 0
+        and green_rec.shape[3] >= 2 * LANES
         and green_rec.shape[3] // shards <= LANES
     )
 

time: 25.8 us -> 24.7 us (0.957)
  Pallas kernels: 25.2 us -> 24.1 us
    pallas_call x1, Pallas kernels: 25.2 us -> 24.1 us  [fused_body(): pl.pallas_call(imaging_kernel, out_shape=jax.ShapeDtypeStruct((1, LANES),...]
where the time goes in v3:
time: 24.7 us; the launch traced here: 24.6 us
  Pallas kernels  24.1 us (98%)
  local copies, waits for them, and re-layouts  0.51 us (2%)
    pallas_call x1, Pallas kernels, fused_body(): pl.pallas_call(imaging_kernel, out_shape=jax.ShapeDtypeStruct((1, LANES),...  24.1 us
    squeeze x1, local copies, waits for them, and re-layouts, fused_body(): return image[0, :points // shards]  0.51 us

profile of v3, /device:TPU:0, one launch (start us, length us, event | category | flops | bytes accessed | tf_op | source)
XLA Modules:
  0.0 24.6 jit_solution(17947005902764263019)
XLA Ops:
  0.0 24.1 %shard_map.55 = f32[1,128]{1,0:T(1,128)S(1)} custom-call(bf16[64,2,8,2048]{3,2,1,0:T(8,128)(2,1)} %bitcast.8, s32[16]{0:T(128)} %refs_1_.1, s32[64,64]{1,0:T(8,128)} %refs_2_.1, bf16[4096,768]{1,0:T(8,128)(2,1)} %bitcast.7, bf16[32,768]{1,0:T(8,128)(2,1)} %bitcast.9), custom_call_target="tpu_custom_call" | custom-call | tf_op jit(solution)/shard_map/pallas_call | solution.py:701
  24.1 0.5 %slice_bitcast_fusion = f32[48]{0:T(128)} fusion(f32[1,128]{1,0:T(1,128)S(1)} %shard_map.55), kind=kLoop, calls=%fused_computation | loop fusion | bytes 384 | tf_op jit(solution)/shard_map/squeeze | solution.py:747

commit v4 on v3

--- a/solution.py
+++ b/solution.py
@@ -62,9 +62,11 @@
 WIDE = 2 * LANES
 PIECE = LANES
 AHEAD = 2
+PLAN = ("M0", "P01", "P12", "P23", "C0", "C1", "A0", "P34", "C2", "N4", "C3", "B0", "C4", "K0", "K1")
 MIXED = True
 MASK = 3.6
 LATE = -0.1
+SPLIT = 1
 
 
 def groups_of(half):
@@ -99,7 +101,7 @@
 
 
 def imaging_kernel(*refs):
-    half = refs[9].shape[0] * LANES
+    half = refs[8].shape[0] * LANES
     chunks = len(chunks_of(half))
     packs = len(groups_of(half))
     dma = pltpu.SemaphoreType.DMA
@@ -139,10 +141,11 @@
     fi_ref,
     x_out,
     x_near,
-    x_far,
     table,
+    p_send,
+    p_recv,
+    near,
     y_send,
-    y_keep,
     y_recv,
     relay_send,
     relay_recv,
@@ -190,7 +193,7 @@
 ):
     shards = i_recv.shape[0]
     cols = shards // (ROWS * CORES)
-    blocks, folds, samples = x_far.shape[:3]
+    blocks, folds, samples = x_near.shape[:3]
     half = blocks * LANES
     length = samples * shards
     steps = chunks_of(half)
@@ -257,18 +260,28 @@
         whole = ref.at[blocks_of(k)]
         pltpu.make_async_copy(whole, whole, sem.at[k]).wait()
 
-    def far_copy(k):
+    def span_of(g):
+        return pl.ds(*packs[g])
+
+    def far_copy(g):
         return remote(
-            x_out.at[blocks_of(k)], x_far.at[blocks_of(k)], far_send, far_recv.at[k], mate
-        )
-
-    def green_load(k, side, part):
+            p_send.at[:, :, :, :, span_of(g)],
+            p_recv.at[:, :, :, :, span_of(g)],
+            far_send,
+            far_recv.at[g],
+            mate,
+        )
+
+    def green_place(lane, side, part):
+        return CORES * 2 * lane + (2 * side + part) * LANES
+
+    def green_load(lane, side, part):
         core_at = core if side == 0 else 1 - core
-        start, size = packs[k]
-        place = CORES * 2 * start + (2 * side + part) * size
-        origin = pl.multiple_of(part * CORES * half + core_at * half + start, LANES)
+        origin = pl.multiple_of(part * CORES * half + core_at * half + lane, LANES)
         return pltpu.make_async_copy(
-            green_ref.at[pl.ds(origin, size), :], green_v.at[pl.ds(place, size), :], green_sem
+            green_ref.at[pl.ds(origin, LANES), :],
+            green_v.at[pl.ds(green_place(lane, side, part), LANES), :],
+            green_sem,
         )
 
     fi_load = pltpu.make_async_copy(fi_hbm, fi_ref, load_sem.at[0])
@@ -285,76 +298,68 @@
     x_load(core, x_near, near_sem, order[-1])
 
     table_rows = 2 * freqs
-    span = CORES * samples
-    line = lax.broadcasted_iota(jnp.int32, (table_rows, span), 0)
-    column = lax.broadcasted_iota(jnp.int32, (table_rows, span), 1)
-    wide = span * SUBLANES
-    spread = lax.broadcasted_iota(jnp.int32, (span, wide), 1) // SUBLANES == lax.broadcasted_iota(
-        jnp.int32, (span, wide), 0
+    line = lax.broadcasted_iota(jnp.int32, (table_rows, samples), 0)
+    column = lax.broadcasted_iota(jnp.int32, (table_rows, samples), 1)
+    spread = lax.broadcasted_iota(jnp.int32, (samples, depth), 1) // SUBLANES == (
+        lax.broadcasted_iota(jnp.int32, (samples, depth), 0)
     )
-    pl.semaphore_wait(barrier, 2 + beside)
-    x_wait(x_out, out_sem, order[0])
-    far_copy(order[0]).start()
     fi_load.wait()
-    bins = jnp.zeros((table_rows, span), jnp.int32)
+    bins = jnp.zeros((table_rows, samples), jnp.int32)
     for side in range(ROWS):
         for leg in range(LEGS):
             for k in range(CORES):
                 to_row = 1 - row if side == 0 else row
                 place = (side * LEGS + leg) * CORES + k
                 bins = jnp.where(line // 2 == place, fi_ref[seat(leg_cols[leg], to_row, k)], bins)
-    time = jnp.where(column < samples, me * samples + column, (mate - 1) * samples + column)
-    angles = lax.rem(bins * time, length).astype(f32) * f32(2.0 * math.pi / length)
+    angles = lax.rem(bins * (me * samples + column), length).astype(f32) * f32(
+        2.0 * math.pi / length
+    )
     small = jnp.where(line % 2 == 0, jnp.cos(angles), -jnp.sin(angles)).astype(bf16)
     stretched = jnp.dot(small, jnp.where(spread, 1.0, 0.0).astype(bf16), preferred_element_type=f32)
-    same_shot = lax.broadcasted_iota(jnp.int32, (SUBLANES, wide), 1) % SUBLANES == (
-        lax.broadcasted_iota(jnp.int32, (SUBLANES, wide), 0)
+    same_shot = lax.broadcasted_iota(jnp.int32, (SUBLANES, depth), 1) % SUBLANES == (
+        lax.broadcasted_iota(jnp.int32, (SUBLANES, depth), 0)
     )
     for r in range(table_rows):
-        spread_row = jnp.broadcast_to(stretched[r : r + 1, :], (SUBLANES, wide))
+        spread_row = jnp.broadcast_to(stretched[r : r + 1, :], (SUBLANES, depth))
         table[r * SUBLANES : (r + 1) * SUBLANES, :] = jnp.where(same_shot, spread_row, 0.0).astype(
             bf16
         )
 
-    tell_line(line_sem.at[0])
-
-    def hand_over(k):
-        x_wait(x_out, out_sem, k)
-        far_copy(k).start()
-
-    hand_over(order[1])
-    map_load.start()
-    src_load.start()
+    def lanes_of(k):
+        return range(packs[k][0], packs[k][0] + packs[k][1], LANES)
 
     def start_green(k):
-        for side in range(CORES):
-            for part in range(2):
-                green_load(k, side, part).start()
-
-    rows = LEGS * CORES * 2 * SUBLANES
-
-    def partial(side, fold, k):
-        start, size = packs[k]
-        total = None
-        for part, ref in enumerate((x_near, x_far)):
+        for lane in lanes_of(k):
+            for side in range(CORES):
+                for part in range(2):
+                    green_load(lane, side, part).start()
+
+    def transform(x_at, ref, g):
+        start, size = packs[g]
+        for fold in range(folds):
             seen = jnp.concatenate(
-                [ref[start // LANES + n, fold].reshape(depth, LANES) for n in range(size // LANES)],
+                [
+                    x_at[start // LANES + n, fold].reshape(depth, LANES)
+                    for n in range(size // LANES)
+                ],
                 axis=1,
             )
-            weights = table[side * rows : (side + 1) * rows, part * depth : (part + 1) * depth]
-            term = jnp.dot(weights, seen, preferred_element_type=f32)
-            total = term if total is None else total + term
-        return total
-
-    def fill(ref, side, k):
-        for fold in range(folds):
-            total = partial(side, fold, k)
-            for leg in range(LEGS):
-                for line_at in range(2 * CORES):
-                    first = (leg * 2 * CORES + line_at) * SUBLANES
-                    ref[leg, line_at * folds + fold, :, pl.ds(*packs[k])] = total[
-                        first : first + SUBLANES
-                    ].astype(ref.dtype)
+            total = jnp.dot(table[...], seen, preferred_element_type=f32)
+            for side in range(ROWS):
+                for leg in range(LEGS):
+                    for line_at in range(2 * CORES):
+                        first = ((side * LEGS + leg) * 2 * CORES + line_at) * SUBLANES
+                        ref[side, leg, line_at * folds + fold, :, span_of(g)] = total[
+                            first : first + SUBLANES
+                        ].astype(ref.dtype)
+
+    def hand_over(g):
+        x_wait(x_out, out_sem, g)
+        transform(x_out, p_send, g)
+
+    def keep_near(g):
+        x_wait(x_near, near_sem, g)
+        transform(x_near, near, g)
 
     def y_copy(leg, k):
         return remote(
@@ -389,16 +394,20 @@
             own_send.at[:, :, at(k)], fin.at[3 * CORES, :, :, at(k)], os_sem, fin_sem.at[k], mate
         )
 
-    def send_partial(k):
-        x_wait(x_near, near_sem, k)
-        far_copy(k).wait_recv()
-        fill(y_send, 0, k)
-
-    def keep_partial(k):
-        fill(y_keep, 1, k)
-        lane = pl.ds(*packs[k])
-        own_send[:, :, lane] = y_keep[LEGS - 1, pick(1 - core), :, lane].astype(bf16)
-        for m in members[k]:
+    def joint(side, leg, lane):
+        return near[side, leg, :, :, lane] + p_recv[side, leg, :, :, lane].astype(f32)
+
+    def send_partial(g):
+        far_copy(g).wait_recv()
+        for leg in range(LEGS):
+            y_send[leg, :, :, span_of(g)] = joint(0, leg, span_of(g)).astype(bf16)
+
+    def keep_partial(g):
+        lane = span_of(g)
+        for leg in range(LEGS):
+            near[1, leg, :, :, lane] = joint(1, leg, lane)
+        own_send[:, :, lane] = near[1, LEGS - 1, pick(1 - core), :, lane].astype(bf16)
+        for m in members[g]:
             own_copy(m).start()
 
     def relay_copy(k):
@@ -412,7 +421,7 @@
 
     def joined(leg, k):
         y_copy(leg, k).wait_recv()
-        return y_keep[leg, :, :, at(k)] + y_recv[leg, :, :, at(k)].astype(f32)
+        return near[1, leg, :, :, at(k)] + y_recv[leg, :, :, at(k)].astype(f32)
 
     def pass_on(k):
         relay_send[:, :, at(k)] = joined(0, k).astype(bf16)
@@ -434,22 +443,17 @@
         )
 
     def send_direct():
-        x_wait(x_near, near_sem, DIRECT)
         far_copy(DIRECT).wait_recv()
-        for side in range(ROWS):
-            for fold in range(folds):
-                total = partial(side, fold, DIRECT)
-                for leg in range(LEGS):
-                    for line_at in range(2 * CORES):
-                        first = (leg * 2 * CORES + line_at) * SUBLANES
-                        place = (side * 2 * CORES + line_at) * folds + fold
-                        value = total[first : first + SUBLANES]
-                        if leg < LEGS - 1:
-                            d_send[leg, place] = value.astype(bf16)
-                        else:
-                            d_keep[place] = value
-        for leg in range(LEGS - 1):
-            direct_copy(leg).start()
+        for leg in range(LEGS):
+            for side in range(ROWS):
+                total = joint(side, leg, span_of(DIRECT))
+                places = pl.ds(side * CORES * groups, CORES * groups)
+                if leg < LEGS - 1:
+                    d_send[leg, places] = total.astype(bf16)
+                else:
+                    d_keep[places] = total
+            if 0 < leg < LEGS - 1:
+                direct_copy(leg).start()
 
     def join_direct():
         pltpu.make_async_copy(d_recv, d_recv, dr_sem).wait()
@@ -490,34 +494,36 @@
     deep = CORES * half // map_v.shape[0]
 
     def mask_chunk(k):
-        start, size = packs[k]
-        for side in range(CORES):
-            core_at = core if side == 0 else 1 - core
-            for i in range(size // deep):
-                seen = mask_v[pl.ds((core_at * half + start) // deep + i, 1), :]
-                seen = jnp.broadcast_to(seen, (deep, points)).astype(bf16)
-                for part in range(2):
-                    place = CORES * 2 * start + (2 * side + part) * size + i * deep
-                    green_v[place : place + deep, :] = green_v[place : place + deep, :] * seen
-
-    def use(k, totals):
-        start, size = packs[k]
-        parts = []
+        for lane in lanes_of(k):
+            for side in range(CORES):
+                core_at = core if side == 0 else 1 - core
+                for i in range(LANES // deep):
+                    seen = mask_v[pl.ds((core_at * half + lane) // deep + i, 1), :]
+                    seen = jnp.broadcast_to(seen, (deep, points)).astype(bf16)
+                    for part in range(2):
+                        place = green_place(lane, side, part) + i * deep
+                        green_v[place : place + deep, :] = green_v[place : place + deep, :] * seen
+
+    def use(start, size, totals):
+        spectra = []
         for total in totals:
             spectrum = total.reshape(block, size) * f32(1.0 / math.sqrt(length))
             turned = jnp.concatenate((spectrum[block // 2 :], -spectrum[: block // 2]), axis=0)
-            parts += [spectrum.astype(bf16), turned.astype(bf16)]
+            spectra += [spectrum.astype(bf16), turned.astype(bf16)]
+        parts = [
+            spectrum[:, lane : lane + LANES] for lane in range(0, size, LANES) for spectrum in spectra
+        ]
         acc[...] += jnp.dot(
             jnp.concatenate(parts, axis=1),
             green_v[CORES * 2 * start : CORES * 2 * (start + size), :],
             preferred_element_type=f32,
         )
 
-    def consume(g):
-        lane = pl.ds(*packs[g])
-        for k in members[g]:
+    def consume(start, size, ks):
+        lane = pl.ds(start, size)
+        for k in ks:
             wait_fin(k)
-        own = y_keep[LEGS - 1, pick(core), :, lane]
+        own = near[1, LEGS - 1, pick(core), :, lane]
         sums = []
         for side in range(CORES):
             total = own if side == 0 else fin[3 * CORES, :, :, lane].astype(f32)
@@ -526,14 +532,14 @@
                 + fin[CORES + side, :, :, lane].astype(f32)
                 + fin[2 * CORES + side, :, :, lane].astype(f32)
             )
-        for k in members[g]:
+        for k in ks:
             wait_last(k)
-        use(g, [sums[side] + fin[side, :, :, lane].astype(f32) for side in range(CORES)])
+        use(start, size, [sums[side] + fin[side, :, :, lane].astype(f32) for side in range(CORES)])
 
     def consume_direct():
         pltpu.make_async_copy(d_fin, d_fin, df_sem).wait()
         use(
-            DIRECT,
+            *packs[DIRECT],
             [
                 d_own[...] + d_fin[1].astype(f32),
                 d_fin[0].astype(f32) + d_fin[2].astype(f32),
@@ -569,25 +575,55 @@
     def flat_of(groups_at):
         return [k for g in groups_at for k in members[g]]
 
-    kept = 0
-    for place, g in enumerate(order):
-        if place + 2 < len(order):
-            hand_over(order[place + 2])
+    def combine(g):
         if g == DIRECT:
-            pl.semaphore_wait(line_sem.at[1], beside)
-            tell(pair_sem, mate)
             send_direct()
-            continue
+            return
         send_partial(g)
         start_y(0, members[g])
         if g == folded[0]:
             start_y(1, members[g])
-            clock = max(clock, 0.85)
+            clock_at_least(0.85)
+
+    def clock_at_least(value):
+        nonlocal clock
+        clock = max(clock, value)
+
+    def advance(token):
+        kind, place = token[:2]
+        g = order[place] if place < len(order) else None
+        if kind == "M":
+            hand_over(g)
+            if place == 0:
+                pl.semaphore_wait(barrier, 2 + beside)
+                tell_line(line_sem.at[0])
+            far_copy(g).start()
+        elif kind == "N":
+            keep_near(g)
+        elif kind == "P":
+            ahead = order[token[2]]
+            x_wait(x_near, near_sem, g)
+            x_wait(x_out, out_sem, ahead)
+            transform(x_out, p_send, ahead)
+            transform(x_near, near, g)
+            far_copy(ahead).start()
+        elif kind == "C":
+            combine(g)
+        elif kind == "K":
+            keep_partial(folded[place])
+        elif kind == "A":
             pl.semaphore_wait(line_sem.at[0], beside)
             tell_line(line_sem.at[1])
-        elif place > 1:
-            keep_partial(folded[kept])
-            kept += 1
+        else:
+            pl.semaphore_wait(line_sem.at[1], beside)
+            tell(pair_sem, mate)
+            direct_copy(0).start()
+
+    for step in PLAN:
+        advance((step[0],) + tuple(int(digit) for digit in step[1:]))
+    kept = sum(step[0] == "K" for step in PLAN)
+    map_load.start()
+    src_load.start()
     for g in range(len(packs)):
         start_green(g)
     turns = [(1, k) for k in flat_of(folded[1:])]
@@ -624,7 +660,10 @@
             mid = max(mid, merged) + 2 * span
             events.append((arrival[2, k], 2, lambda k=k: close(k)))
             done = max(mid + hop + 0.5, arrival[2, k] + span + hop, arrival[LEGS - 1, k], done)
-        events.append((done, 4, lambda g=g: consume(g)))
+            if g in folded[len(folded) - SPLIT :]:
+                events.append((done, 4, lambda k=k: consume(*steps[k], [k])))
+        if g not in folded[len(folded) - SPLIT :]:
+            events.append((done, 4, lambda g=g: consume(*packs[g], members[g])))
     events.append((done + LATE, 9, consume_direct))
     for g in range(len(packs)):
         events.append((MASK + 0.4 + 0.6 * g, 6, lambda g=g: mask_chunk(g)))
@@ -660,7 +699,7 @@
     others = i_recv.at[pl.ds(0, shards - 1)]
     rest = pl.ds(0, half - packs[DIRECT][1])
     for sent, sem in (
-        (x_out, far_send),
+        (p_send, far_send),
         (y_send.at[:, :, :, rest], ys_sem),
         (relay_send.at[:, :, rest], rs_sem),
         (cross_send.at[:, :, rest], cs_sem),
@@ -676,7 +715,7 @@
     first = jnp.minimum(me * each // LANES, points // LANES - 2) * LANES
     total = jnp.broadcast_to(total, (SUBLANES, 2 * LANES))
     shift = lax.rem(2 * LANES - (me * each - first), 2 * LANES)
-    out_ref[...] = pltpu.roll(total, shift, 1)[0:1, :LANES]
+    out_ref[...] = pltpu.roll(total, shift, 1)[0:1, :each]
     pltpu.make_async_copy(others, others, is_sem).wait()
 
 
@@ -700,17 +739,18 @@
     direct = (ROWS * CORES * groups, SUBLANES, groups_of(half)[DIRECT][1])
     image = pl.pallas_call(
         imaging_kernel,
-        out_shape=jax.ShapeDtypeStruct((1, LANES), f32),
+        out_shape=jax.ShapeDtypeStruct((1, points // shards), f32),
         in_specs=[outside] * 5,
         out_specs=pl.BlockSpec(memory_space=pltpu.VMEM),
         scratch_shapes=[
             pltpu.SMEM(freq_index.shape, jnp.int32),
             pltpu.VMEM((half // LANES, folds, samples, SUBLANES, LANES), bf16),
             pltpu.VMEM((half // LANES, folds, samples, SUBLANES, LANES), bf16),
-            pltpu.VMEM((half // LANES, folds, samples, SUBLANES, LANES), bf16),
-            pltpu.VMEM((2 * freqs * SUBLANES, CORES * samples * SUBLANES), bf16),
+            pltpu.VMEM((2 * freqs * SUBLANES, samples * SUBLANES), bf16),
+            pltpu.VMEM((ROWS, LEGS) + piece, bf16),
+            pltpu.VMEM((ROWS, LEGS) + piece, bf16),
+            pltpu.VMEM((ROWS, LEGS) + piece, f32),
             pltpu.VMEM((LEGS,) + piece, bf16),
-            pltpu.VMEM((LEGS,) + piece, f32),
             pltpu.VMEM((LEGS - 1,) + piece, bf16),
             pltpu.VMEM(piece, bf16),
             pltpu.VMEM(piece, bf16),
@@ -744,7 +784,7 @@
             for array in (records, freq_index, block_map, green, sources)
         )
     )
-    return image[0, : points // shards]
+    return image.reshape(points // shards)
 
 
 def moves_less(traces, freq_index, block_map, green_rec):

time: 24.7 us -> 23.8 us (0.964)
  Pallas kernels: 24.1 us -> 23.1 us
    pallas_call x1, Pallas kernels: 24.1 us -> 23.1 us  [fused_body(): pl.pallas_call(imaging_kernel, out_shape=jax.ShapeDtypeStruct((1, points...]
    squeeze x1 -> x0, local copies, waits for them, and re-layouts: 0.51 us -> none  [fused_body(): return image[0, :points // shards]]
    unnamed x0 -> x1, local copies, waits for them, and re-layouts: none -> 0.51 us
where the time goes in v4:
time: 23.8 us; the launch traced here: 23.6 us
  Pallas kernels  23.1 us (97%)
  local copies, waits for them, and re-layouts  0.51 us (2%)
    pallas_call x1, Pallas kernels, fused_body(): pl.pallas_call(imaging_kernel, out_shape=jax.ShapeDtypeStruct((1, points...  23.1 us
    unnamed x1, local copies, waits for them, and re-layouts  0.51 us

profile of v4, /device:TPU:0, one launch (start us, length us, event | category | flops | bytes accessed | tf_op | source)
XLA Modules:
  0.0 23.6 jit_solution(17732355805251021321)
XLA Ops:
  0.0 23.1 %shard_map.55 = f32[1,48]{1,0:T(1,128)S(1)} custom-call(bf16[64,2,8,2048]{3,2,1,0:T(8,128)(2,1)} %bitcast.8, s32[16]{0:T(128)} %refs_1_.1, s32[64,64]{1,0:T(8,128)} %refs_2_.1, bf16[4096,768]{1,0:T(8,128)(2,1)} %bitcast.7, bf16[32,768]{1,0:T(8,128)(2,1)} %bitcast.9), custom_call_target="tpu_custom_call" | custom-call | tf_op jit(solution)/shard_map/pallas_call | solution.py:740
  23.1 0.5 %copy.7 = f32[48]{0:T(128)} copy(f32[48]{0:T(128)S(1)} %bitcast.6) | data formatting | bytes 384

commit v5 on v4

--- a/solution.py
+++ b/solution.py
@@ -67,6 +67,7 @@
 MASK = 3.6
 LATE = -0.1
 SPLIT = 1
+LEAD = 0
 
 
 def groups_of(half):
@@ -509,15 +510,19 @@
         for total in totals:
             spectrum = total.reshape(block, size) * f32(1.0 / math.sqrt(length))
             turned = jnp.concatenate((spectrum[block // 2 :], -spectrum[: block // 2]), axis=0)
-            spectra += [spectrum.astype(bf16), turned.astype(bf16)]
+            spectra += [spectrum, turned]
         parts = [
             spectrum[:, lane : lane + LANES] for lane in range(0, size, LANES) for spectrum in spectra
         ]
-        acc[...] += jnp.dot(
-            jnp.concatenate(parts, axis=1),
+        whole = jnp.concatenate(parts, axis=1)
+        high = whole.astype(bf16)
+        low = (whole - high.astype(f32)).astype(bf16)
+        both = jnp.dot(
+            jnp.concatenate((high, low), axis=0),
             green_v[CORES * 2 * start : CORES * 2 * (start + size), :],
             preferred_element_type=f32,
         )
+        acc[...] += both[:block] + both[block:]
 
     def consume(start, size, ks):
         lane = pl.ds(start, size)
@@ -629,7 +634,9 @@
     turns = [(1, k) for k in flat_of(folded[1:])]
     others = [(2, k) for k in flat_of(folded)]
     if MIXED:
-        turns = [t for pair in zip(turns, others) for t in pair] + others[len(turns) :]
+        led = turns[LEAD:]
+        mixed = [t for pair in zip(others, led) for t in pair]
+        turns = turns[:LEAD] + mixed + others[len(led) :]
     else:
         turns += others
     for leg, k in turns:
@@ -682,20 +689,14 @@
         first = jnp.minimum(d * each // LANES, points // LANES - 2)
         return pl.ds(pl.multiple_of(first * LANES, LANES), 2 * LANES)
 
-    peers = []
-    for leg_col in leg_cols:
-        for to_row in (1 - row, row):
-            for to_core in (1 - core, core):
-                peers.append(seat(leg_col, to_row, to_core))
-
-    def i_copy(slot):
-        to = peers[slot]
-        return remote(flat.at[:, window(to)], i_recv.at[slot], is_sem, ir_sem, to)
+    def i_copy(place):
+        to = place + jnp.minimum(jnp.maximum(place + 1 - me, 0), 1)
+        return remote(flat.at[:, window(to)], i_recv.at[me], is_sem, ir_sem, to)
 
     pl.semaphore_wait(row_sem, 1)
-    for slot in range(shards - 1):
-        i_copy(slot).start()
-    total = flat[:, window(me)]
+    for place in range(shards - 1):
+        i_copy(place).start()
+    i_recv[me] = flat[:, window(me)]
     others = i_recv.at[pl.ds(0, shards - 1)]
     rest = pl.ds(0, half - packs[DIRECT][1])
     for sent, sem in (
@@ -710,7 +711,8 @@
     ):
         pltpu.make_async_copy(sent, sent, sem).wait()
     pltpu.make_async_copy(others, others, ir_sem).wait()
-    for slot in range(shards - 1):
+    total = i_recv[0]
+    for slot in range(1, shards):
         total = total + i_recv[slot]
     first = jnp.minimum(me * each // LANES, points // LANES - 2) * LANES
     total = jnp.broadcast_to(total, (SUBLANES, 2 * LANES))

time: 23.8 us -> 23.6 us (level)
  no operation moved by 1% of the time
where the time goes in v5:
time: 23.6 us; the launch traced here: 23.5 us
  Pallas kernels  22.9 us (97%)
  local copies, waits for them, and re-layouts  0.51 us (2%)
    pallas_call x1, Pallas kernels, fused_body(): pl.pallas_call(imaging_kernel, out_shape=jax.ShapeDtypeStruct((1, points...  22.9 us
    unnamed x1, local copies, waits for them, and re-layouts  0.51 us

profile of v5, /device:TPU:0, one launch (start us, length us, event | category | flops | bytes accessed | tf_op | source)
XLA Modules:
  0.0 23.5 jit_solution(11355320680325162432)
XLA Ops:
  0.0 22.9 %shard_map.55 = f32[1,48]{1,0:T(1,128)S(1)} custom-call(bf16[64,2,8,2048]{3,2,1,0:T(8,128)(2,1)} %bitcast.8, s32[16]{0:T(128)} %refs_1_.1, s32[64,64]{1,0:T(8,128)} %refs_2_.1, bf16[4096,768]{1,0:T(8,128)(2,1)} %bitcast.7, bf16[32,768]{1,0:T(8,128)(2,1)} %bitcast.9), custom_call_target="tpu_custom_call" | custom-call | tf_op jit(solution)/shard_map/pallas_call | solution.py:742
  23.0 0.5 %copy.7 = f32[48]{0:T(128)} copy(f32[48]{0:T(128)S(1)} %bitcast.6) | data formatting | bytes 384

commit v6 on v5

--- a/solution.py
+++ b/solution.py
@@ -629,8 +629,6 @@
     kept = sum(step[0] == "K" for step in PLAN)
     map_load.start()
     src_load.start()
-    for g in range(len(packs)):
-        start_green(g)
     turns = [(1, k) for k in flat_of(folded[1:])]
     others = [(2, k) for k in flat_of(folded)]
     if MIXED:
@@ -654,6 +652,8 @@
     for k in tail:
         expect(LEGS - 1, k)
     events = [(6.2, 7, send_last), (MASK, 5, make_mask)]
+    for g in range(len(packs)):
+        events.append((0.3 + 0.3 * g, 3, lambda g=g: start_green(g)))
     for place, g in enumerate(folded[kept:]):
         events.append((max(arrival[0, members[g][0]] - 0.6, 0.4), 8, lambda g=g: keep_partial(g)))
     mid = 0.0

time: 23.6 us -> 23.6 us (level)
  no operation moved by 1% of the time
where the time goes in v6:
time: 23.6 us; the launch traced here: 23.5 us
  Pallas kernels  23 us (97%)
  local copies, waits for them, and re-layouts  0.51 us (2%)
    pallas_call x1, Pallas kernels, fused_body(): pl.pallas_call(imaging_kernel, out_shape=jax.ShapeDtypeStruct((1, points...  23 us
    unnamed x1, local copies, waits for them, and re-layouts  0.51 us

profile of v6, /device:TPU:0, one launch (start us, length us, event | category | flops | bytes accessed | tf_op | source)
XLA Modules:
  0.0 23.5 jit_solution(8388331533474904651)
XLA Ops:
  0.0 23.0 %shard_map.55 = f32[1,48]{1,0:T(1,128)S(1)} custom-call(bf16[64,2,8,2048]{3,2,1,0:T(8,128)(2,1)} %bitcast.8, s32[16]{0:T(128)} %refs_1_.1, s32[64,64]{1,0:T(8,128)} %refs_2_.1, bf16[4096,768]{1,0:T(8,128)(2,1)} %bitcast.7, bf16[32,768]{1,0:T(8,128)(2,1)} %bitcast.9), custom_call_target="tpu_custom_call" | custom-call | tf_op jit(solution)/shard_map/pallas_call | solution.py:742
  23.0 0.5 %copy.7 = f32[48]{0:T(128)} copy(f32[48]{0:T(128)S(1)} %bitcast.6) | data formatting | bytes 384
